TPU v7x, 32 devices: a whole 2x2x4 slice. The times are simulated.
32 devices in a mesh: model: 8 (over z, y), data: 4 (over x, core).
Axes of the slice: x: 2, y: 2, z: 4, core: 2. Of those that a mesh axis runs over, the one named last changes fastest.
Arguments:
- x_tokens: bfloat16 [32, 49, 768], P('data')
- y_target: bfloat16 [32, 49, 768], P('data')
- w_in: float32 [12, 768, 3072], P(None, None, 'model')
- w_out: float32 [12, 3072, 768], P(None, 'model')
Outputs:
- output 1: float32 [12, 768, 3072], P(None, None, 'model')
- output 2: float32 [12, 3072, 768], P(None, 'model')
- output 3: float32 [], replicated
All inputs are finite; a program needn't handle non-finite values.
Results may differ from a plain program's by a relative error of at most 0.00413934.
Values are sent between devices in bfloat16 or wider.
A program may use at most 1 GiB of HBM per device.

v0:
```python
import math
import jax
import jax.numpy as jnp
from jax import lax
from jax.sharding import PartitionSpec as P

RHO_SCALE = 0.5
ETA = 1.0
CONTRACT_ROWS = (((0,), (0,)), ((), ()))
CONTRACT_COLS = (((1,), (1,)), ((), ()))


def gelu_fn(values):
    return jax.nn.gelu(values, approximate=True)


def train_pass(w_in_b, w_out_b, x_local, y_local, n_data):
    layers = len(w_in_b)
    saved_acts = []
    hidden = x_local
    for layer_idx in range(layers):
        z_round = jnp.dot(hidden, w_in_b[layer_idx], preferred_element_type=jnp.float32).astype(jnp.bfloat16)
        act_val, act_pull = jax.vjp(gelu_fn, z_round.astype(jnp.float32))
        act_b = act_val.astype(jnp.bfloat16)
        mix_part = jnp.dot(act_b, w_out_b[layer_idx], preferred_element_type=jnp.float32)
        saved_acts.append((hidden, act_b, act_pull))
        hidden = (hidden.astype(jnp.float32) + lax.psum(mix_part, "model")).astype(jnp.bfloat16)
    residual = hidden.astype(jnp.float32) - y_local.astype(jnp.float32)
    loss_part = 0.5 * jnp.sum(residual * residual)
    grad_h = residual / residual.size
    grads_in = [None] * layers
    grads_out = [None] * layers
    for layer_idx in reversed(range(layers)):
        hid_in, act_b, act_pull = saved_acts[layer_idx]
        grad_b = grad_h.astype(jnp.bfloat16)
        g_out_loc = lax.dot_general(act_b, grad_b, CONTRACT_ROWS, preferred_element_type=jnp.float32).astype(jnp.bfloat16)
        act_grad = lax.dot_general(grad_b, w_out_b[layer_idx], CONTRACT_COLS, preferred_element_type=jnp.float32)
        dz_round = act_pull(act_grad)[0].astype(jnp.bfloat16)
        g_in_loc = lax.dot_general(hid_in, dz_round, CONTRACT_ROWS, preferred_element_type=jnp.float32).astype(jnp.bfloat16)
        if layer_idx > 0:
            back_part = lax.dot_general(dz_round, w_in_b[layer_idx], CONTRACT_COLS, preferred_element_type=jnp.float32)
            grad_h = grad_h + lax.psum(back_part, "model")
        sum_in, sum_out = lax.psum((g_in_loc.astype(jnp.float32), g_out_loc.astype(jnp.float32)), "data")
        grads_in[layer_idx] = sum_in / n_data
        grads_out[layer_idx] = sum_out / n_data
    return loss_part, grads_in, grads_out


def solution(mesh):
    n_data = mesh.shape["data"]
    act_spec = P("data", None, None)
    in_spec = P(None, None, "model")
    out_spec = P(None, "model", None)

    def sam_step(x_tokens, y_target, w_in, w_out):
        rho = RHO_SCALE * math.sqrt(x_tokens.shape[-1] / w_in.shape[-1])
        elem_total = x_tokens.size

        def local_step(x_blk, y_blk, win_loc, wout_loc):
            layers = win_loc.shape[0]
            x_flat = x_blk.reshape(-1, x_blk.shape[-1])
            y_flat = y_blk.reshape(-1, y_blk.shape[-1])
            base_in = [win_loc[layer_idx].astype(jnp.bfloat16) for layer_idx in range(layers)]
            base_out = [wout_loc[layer_idx].astype(jnp.bfloat16) for layer_idx in range(layers)]
            first_pass = train_pass(base_in, base_out, x_flat, y_flat, n_data)
            grad_in = first_pass[1]
            grad_out = first_pass[2]
            sq_part = jnp.zeros((), jnp.float32)
            for layer_idx in range(layers):
                sq_part = sq_part + jnp.sum(grad_in[layer_idx] * grad_in[layer_idx]) + jnp.sum(grad_out[layer_idx] * grad_out[layer_idx])
            step_scale = rho / jnp.sqrt(lax.psum(sq_part, "model"))
            pert_in = [(win_loc[layer_idx] + step_scale * grad_in[layer_idx]).astype(jnp.bfloat16) for layer_idx in range(layers)]
            pert_out = [(wout_loc[layer_idx] + step_scale * grad_out[layer_idx]).astype(jnp.bfloat16) for layer_idx in range(layers)]
            loss_part, pgrad_in, pgrad_out = train_pass(pert_in, pert_out, x_flat, y_flat, n_data)
            loss_val = lax.psum(loss_part, "data") / elem_total
            new_in = win_loc - ETA * jnp.stack(pgrad_in)
            new_out = wout_loc - ETA * jnp.stack(pgrad_out)
            return new_in, new_out, loss_val

        stepper = jax.shard_map(local_step, mesh=mesh, in_specs=(act_spec, act_spec, in_spec, out_spec), out_specs=(in_spec, out_spec, P()), check_vma=False)
        return stepper(x_tokens, y_target, w_in, w_out)

    return sam_step
```

profile of v0, /device:TPU:31, one launch (start us, length us, event | category | flops | bytes accessed | tf_op | source)
XLA Modules:
  0.0 5127.5 jit_solution(15273756696555285986)
XLA Ops:
  28.7 81.0 %all-reduce.51.cloned.1.call-done = f32[392,768]{1,0:T(8,128)} async-done(((f32[392,768]{1,0:T(8,128)}), f32[392,768]{1,0:T(8,128)}) %all-reduce.51.cloned.1.call-update) | async-done | bytes 1204240 | tf_op jit(solution)/shard_map/psum | solution.py:27
  116.2 80.8 %all-reduce.53.cloned.1.call-done = f32[392,768]{1,0:T(8,128)} async-done(((f32[392,768]{1,0:T(8,128)}), f32[392,768]{1,0:T(8,128)}) %all-reduce.53.cloned.1.call-update) | async-done | bytes 1204240 | tf_op jit(solution)/shard_map/psum | solution.py:27
  203.6 80.8 %all-reduce.55.cloned.1.call-done = f32[392,768]{1,0:T(8,128)} async-done(((f32[392,768]{1,0:T(8,128)}), f32[392,768]{1,0:T(8,128)}) %all-reduce.55.cloned.1.call-update) | async-done | bytes 1204240 | tf_op jit(solution)/shard_map/psum | solution.py:27
  291.1 80.8 %all-reduce.57.cloned.1.call-done = f32[392,768]{1,0:T(8,128)} async-done(((f32[392,768]{1,0:T(8,128)}), f32[392,768]{1,0:T(8,128)}) %all-reduce.57.cloned.1.call-update) | async-done | bytes 1204240 | tf_op jit(solution)/shard_map/psum | solution.py:27
  378.5 80.9 %all-reduce.59.cloned.1.call-done = f32[392,768]{1,0:T(8,128)} async-done(((f32[392,768]{1,0:T(8,128)}), f32[392,768]{1,0:T(8,128)}) %all-reduce.59.cloned.1.call-update) | async-done | bytes 1204240 | tf_op jit(solution)/shard_map/psum | solution.py:27
  466.0 80.8 %all-reduce.61.cloned.1.call-done = f32[392,768]{1,0:T(8,128)} async-done(((f32[392,768]{1,0:T(8,128)}), f32[392,768]{1,0:T(8,128)}) %all-reduce.61.cloned.1.call-update) | async-done | bytes 1204240 | tf_op jit(solution)/shard_map/psum | solution.py:27
  553.4 80.8 %all-reduce.63.cloned.1.call-done = f32[392,768]{1,0:T(8,128)} async-done(((f32[392,768]{1,0:T(8,128)}), f32[392,768]{1,0:T(8,128)}) %all-reduce.63.cloned.1.call-update) | async-done | bytes 1204240 | tf_op jit(solution)/shard_map/psum | solution.py:27
  640.8 80.8 %all-reduce.65.cloned.1.call-done = f32[392,768]{1,0:T(8,128)} async-done(((f32[392,768]{1,0:T(8,128)}), f32[392,768]{1,0:T(8,128)}) %all-reduce.65.cloned.1.call-update) | async-done | bytes 1204240 | tf_op jit(solution)/shard_map/psum | solution.py:27
  728.3 80.8 %all-reduce.67.cloned.1.call-done = f32[392,768]{1,0:T(8,128)} async-done(((f32[392,768]{1,0:T(8,128)}), f32[392,768]{1,0:T(8,128)}) %all-reduce.67.cloned.1.call-update) | async-done | bytes 1204240 | tf_op jit(solution)/shard_map/psum | solution.py:27
  815.7 80.8 %all-reduce.69.cloned.1.call-done = f32[392,768]{1,0:T(8,128)} async-done(((f32[392,768]{1,0:T(8,128)}), f32[392,768]{1,0:T(8,128)}) %all-reduce.69.cloned.1.call-update) | async-done | bytes 1204240 | tf_op jit(solution)/shard_map/psum | solution.py:27
  903.3 80.6 %all-reduce.71.cloned.1.call-done = f32[392,768]{1,0:T(8,128)} async-done(((f32[392,768]{1,0:T(8,128)}), f32[392,768]{1,0:T(8,128)}) %all-reduce.71.cloned.1.call-update) | async-done | bytes 1204240 | tf_op jit(solution)/shard_map/psum | solution.py:27
  994.0 77.1 %all-reduce.73.cloned.1.call-done = f32[392,768]{1,0:T(8,128)} async-done(((f32[392,768]{1,0:T(8,128)}), f32[392,768]{1,0:T(8,128)}) %all-reduce.73.cloned.1.call-update) | async-done | bytes 1204240 | tf_op jit(solution)/shard_map/psum | solution.py:27
  1078.6 80.9 %all-reduce.75.cloned.1.call-done = f32[392,768]{1,0:T(8,128)} async-done(((f32[392,768]{1,0:T(8,128)}), f32[392,768]{1,0:T(8,128)}) %all-reduce.75.cloned.1.call-update) | async-done | bytes 1204240 | tf_op jit(solution)/shard_map/psum | solution.py:42
  1166.9 80.8 %all-reduce.77.cloned.1.call-done = f32[392,768]{1,0:T(8,128)} async-done(((f32[392,768]{1,0:T(8,128)}), f32[392,768]{1,0:T(8,128)}) %all-reduce.77.cloned.1.call-update) | async-done | bytes 1204240 | tf_op jit(solution)/shard_map/psum | solution.py:42
  1255.5 80.8 %all-reduce.79.cloned.1.call-done = f32[392,768]{1,0:T(8,128)} async-done(((f32[392,768]{1,0:T(8,128)}), f32[392,768]{1,0:T(8,128)}) %all-reduce.79.cloned.1.call-update) | async-done | bytes 1204240 | tf_op jit(solution)/shard_map/psum | solution.py:42
  1344.2 80.8 %all-reduce.81.cloned.1.call-done = f32[392,768]{1,0:T(8,128)} async-done(((f32[392,768]{1,0:T(8,128)}), f32[392,768]{1,0:T(8,128)}) %all-reduce.81.cloned.1.call-update) | async-done | bytes 1204240 | tf_op jit(solution)/shard_map/psum | solution.py:42
  1433.0 80.8 %all-reduce.83.cloned.1.call-done = f32[392,768]{1,0:T(8,128)} async-done(((f32[392,768]{1,0:T(8,128)}), f32[392,768]{1,0:T(8,128)}) %all-reduce.83.cloned.1.call-update) | async-done | bytes 1204240 | tf_op jit(solution)/shard_map/psum | solution.py:42
  1521.7 80.8 %all-reduce.85.cloned.1.call-done = f32[392,768]{1,0:T(8,128)} async-done(((f32[392,768]{1,0:T(8,128)}), f32[392,768]{1,0:T(8,128)}) %all-reduce.85.cloned.1.call-update) | async-done | bytes 1204240 | tf_op jit(solution)/shard_map/psum | solution.py:42
  1614.5 76.7 %all-reduce.87.cloned.1.call-done = f32[392,768]{1,0:T(8,128)} async-done(((f32[392,768]{1,0:T(8,128)}), f32[392,768]{1,0:T(8,128)}) %all-reduce.87.cloned.1.call-update) | async-done | bytes 1204240 | tf_op jit(solution)/shard_map/psum | solution.py:42
  1708.1 71.5 %all-reduce.89.cloned.1.call-done = f32[392,768]{1,0:T(8,128)} async-done(((f32[392,768]{1,0:T(8,128)}), f32[392,768]{1,0:T(8,128)}) %all-reduce.89.cloned.1.call-update) | async-done | bytes 1204240 | tf_op jit(solution)/shard_map/psum | solution.py:42
  1797.7 70.7 %all-reduce.91.cloned.1.call-done = f32[392,768]{1,0:T(8,128)} async-done(((f32[392,768]{1,0:T(8,128)}), f32[392,768]{1,0:T(8,128)}) %all-reduce.91.cloned.1.call-update) | async-done | bytes 1204240 | tf_op jit(solution)/shard_map/psum | solution.py:42
  1886.4 70.8 %all-reduce.93.cloned.1.call-done = f32[392,768]{1,0:T(8,128)} async-done(((f32[392,768]{1,0:T(8,128)}), f32[392,768]{1,0:T(8,128)}) %all-reduce.93.cloned.1.call-update) | async-done | bytes 1204240 | tf_op jit(solution)/shard_map/psum | solution.py:42
  1974.8 70.7 %all-reduce.95.cloned.1.call-done = f32[392,768]{1,0:T(8,128)} async-done(((f32[392,768]{1,0:T(8,128)}), f32[392,768]{1,0:T(8,128)}) %all-reduce.95.cloned.1.call-update) | async-done | bytes 1204240 | tf_op jit(solution)/shard_map/psum | solution.py:42
  2053.3 474.4 %all-reduce.145.cloned.1.call-done = (f32[768,384]{0,1:T(8,128)}, f32[384,768]{1,0:T(8,128)}, f32[768,384]{0,1:T(8,128)}, f32[384,768]{1,0:T(8,128)}, f32[768,38...) async-done(((f32[768,384]{0,1:T(8,128)}, ...) | async-done | bytes 28311568 | tf_op jit(solution)/shard_map/psum | solution.py:43
  2603.1 81.4 %all-reduce.97.cloned.1.call-done = f32[392,768]{1,0:T(8,128)} async-done(((f32[392,768]{1,0:T(8,128)}), f32[392,768]{1,0:T(8,128)}) %all-reduce.97.cloned.1.call-update) | async-done | bytes 1204240 | tf_op jit(solution)/shard_map/psum | solution.py:27
  2688.9 80.9 %all-reduce.99.cloned.1.call-done = f32[392,768]{1,0:T(8,128)} async-done(((f32[392,768]{1,0:T(8,128)}), f32[392,768]{1,0:T(8,128)}) %all-reduce.99.cloned.1.call-update) | async-done | bytes 1204240 | tf_op jit(solution)/shard_map/psum | solution.py:27
  2785.3 71.1 %all-reduce.101.cloned.1.call-done = f32[392,768]{1,0:T(8,128)} async-done(((f32[392,768]{1,0:T(8,128)}), f32[392,768]{1,0:T(8,128)}) %all-reduce.101.cloned.1.call-update) | async-done | bytes 1204240 | tf_op jit(solution)/shard_map/psum | solution.py:27
  2860.9 80.9 %all-reduce.103.cloned.1.call-done = f32[392,768]{1,0:T(8,128)} async-done(((f32[392,768]{1,0:T(8,128)}), f32[392,768]{1,0:T(8,128)}) %all-reduce.103.cloned.1.call-update) | async-done | bytes 1204240 | tf_op jit(solution)/shard_map/psum | solution.py:27
  2948.0 80.4 %all-reduce.105.cloned.1.call-done = f32[392,768]{1,0:T(8,128)} async-done(((f32[392,768]{1,0:T(8,128)}), f32[392,768]{1,0:T(8,128)}) %all-reduce.105.cloned.1.call-update) | async-done | bytes 1204240 | tf_op jit(solution)/shard_map/psum | solution.py:27
  3034.1 80.9 %all-reduce.107.cloned.1.call-done = f32[392,768]{1,0:T(8,128)} async-done(((f32[392,768]{1,0:T(8,128)}), f32[392,768]{1,0:T(8,128)}) %all-reduce.107.cloned.1.call-update) | async-done | bytes 1204240 | tf_op jit(solution)/shard_map/psum | solution.py:27
  3120.7 80.8 %all-reduce.109.cloned.1.call-done = f32[392,768]{1,0:T(8,128)} async-done(((f32[392,768]{1,0:T(8,128)}), f32[392,768]{1,0:T(8,128)}) %all-reduce.109.cloned.1.call-update) | async-done | bytes 1204240 | tf_op jit(solution)/shard_map/psum | solution.py:27
  3211.9 76.3 %all-reduce.111.cloned.1.call-done = f32[392,768]{1,0:T(8,128)} async-done(((f32[392,768]{1,0:T(8,128)}), f32[392,768]{1,0:T(8,128)}) %all-reduce.111.cloned.1.call-update) | async-done | bytes 1204240 | tf_op jit(solution)/shard_map/psum | solution.py:27
  3292.7 80.8 %all-reduce.113.cloned.1.call-done = f32[392,768]{1,0:T(8,128)} async-done(((f32[392,768]{1,0:T(8,128)}), f32[392,768]{1,0:T(8,128)}) %all-reduce.113.cloned.1.call-update) | async-done | bytes 1204240 | tf_op jit(solution)/shard_map/psum | solution.py:27
  3379.2 80.8 %all-reduce.115.cloned.1.call-done = f32[392,768]{1,0:T(8,128)} async-done(((f32[392,768]{1,0:T(8,128)}), f32[392,768]{1,0:T(8,128)}) %all-reduce.115.cloned.1.call-update) | async-done | bytes 1204240 | tf_op jit(solution)/shard_map/psum | solution.py:27
  3465.8 80.8 %all-reduce.117.cloned.1.call-done = f32[392,768]{1,0:T(8,128)} async-done(((f32[392,768]{1,0:T(8,128)}), f32[392,768]{1,0:T(8,128)}) %all-reduce.117.cloned.1.call-update) | async-done | bytes 1204240 | tf_op jit(solution)/shard_map/psum | solution.py:27
  3551.8 80.9 %all-reduce.119.cloned.1.call-done = f32[392,768]{1,0:T(8,128)} async-done(((f32[392,768]{1,0:T(8,128)}), f32[392,768]{1,0:T(8,128)}) %all-reduce.119.cloned.1.call-update) | async-done | bytes 1204240 | tf_op jit(solution)/shard_map/psum | solution.py:27
  3638.7 80.8 %all-reduce.121.cloned.1.call-done = f32[392,768]{1,0:T(8,128)} async-done(((f32[392,768]{1,0:T(8,128)}), f32[392,768]{1,0:T(8,128)}) %all-reduce.121.cloned.1.call-update) | async-done | bytes 1204240 | tf_op jit(solution)/shard_map/psum | solution.py:42
  3724.6 80.8 %all-reduce.123.cloned.1.call-done = f32[392,768]{1,0:T(8,128)} async-done(((f32[392,768]{1,0:T(8,128)}), f32[392,768]{1,0:T(8,128)}) %all-reduce.123.cloned.1.call-update) | async-done | bytes 1204240 | tf_op jit(solution)/shard_map/psum | solution.py:42
  3812.2 80.6 %all-reduce.125.cloned.1.call-done = f32[392,768]{1,0:T(8,128)} async-done(((f32[392,768]{1,0:T(8,128)}), f32[392,768]{1,0:T(8,128)}) %all-reduce.125.cloned.1.call-update) | async-done | bytes 1204240 | tf_op jit(solution)/shard_map/psum | solution.py:42
  3899.4 80.8 %all-reduce.127.cloned.1.call-done = f32[392,768]{1,0:T(8,128)} async-done(((f32[392,768]{1,0:T(8,128)}), f32[392,768]{1,0:T(8,128)}) %all-reduce.127.cloned.1.call-update) | async-done | bytes 1204240 | tf_op jit(solution)/shard_map/psum | solution.py:42
  3986.3 80.8 %all-reduce.129.cloned.1.call-done = f32[392,768]{1,0:T(8,128)} async-done(((f32[392,768]{1,0:T(8,128)}), f32[392,768]{1,0:T(8,128)}) %all-reduce.129.cloned.1.call-update) | async-done | bytes 1204240 | tf_op jit(solution)/shard_map/psum | solution.py:42
  4072.0 80.8 %all-reduce.131.cloned.1.call-done = f32[392,768]{1,0:T(8,128)} async-done(((f32[392,768]{1,0:T(8,128)}), f32[392,768]{1,0:T(8,128)}) %all-reduce.131.cloned.1.call-update) | async-done | bytes 1204240 | tf_op jit(solution)/shard_map/psum | solution.py:42
  4162.7 76.3 %all-reduce.133.cloned.1.call-done = f32[392,768]{1,0:T(8,128)} async-done(((f32[392,768]{1,0:T(8,128)}), f32[392,768]{1,0:T(8,128)}) %all-reduce.133.cloned.1.call-update) | async-done | bytes 1204240 | tf_op jit(solution)/shard_map/psum | solution.py:42
  4253.4 71.6 %all-reduce.135.cloned.1.call-done = f32[392,768]{1,0:T(8,128)} async-done(((f32[392,768]{1,0:T(8,128)}), f32[392,768]{1,0:T(8,128)}) %all-reduce.135.cloned.1.call-update) | async-done | bytes 1204240 | tf_op jit(solution)/shard_map/psum | solution.py:42
  4339.4 71.3 %all-reduce.137.cloned.1.call-done = f32[392,768]{1,0:T(8,128)} async-done(((f32[392,768]{1,0:T(8,128)}), f32[392,768]{1,0:T(8,128)}) %all-reduce.137.cloned.1.call-update) | async-done | bytes 1204240 | tf_op jit(solution)/shard_map/psum | solution.py:42
  4425.5 71.4 %all-reduce.139.cloned.1.call-done = f32[392,768]{1,0:T(8,128)} async-done(((f32[392,768]{1,0:T(8,128)}), f32[392,768]{1,0:T(8,128)}) %all-reduce.139.cloned.1.call-update) | async-done | bytes 1204240 | tf_op jit(solution)/shard_map/psum | solution.py:42
  4510.7 71.7 %all-reduce.141.cloned.1.call-done = f32[392,768]{1,0:T(8,128)} async-done(((f32[392,768]{1,0:T(8,128)}), f32[392,768]{1,0:T(8,128)}) %all-reduce.141.cloned.1.call-update) | async-done | bytes 1204240 | tf_op jit(solution)/shard_map/psum | solution.py:42
  4597.2 467.0 %all-reduce.143.cloned.1.call-done = (f32[768,384]{0,1:T(8,128)}, f32[768,384]{0,1:T(8,128)}, f32[768,384]{0,1:T(8,128)}, f32[768,384]{0,1:T(8,128)}, f32[768,38...) async-done(((f32[768,384]{0,1:T(8,128)}, ...) | async-done | bytes 28311568 | tf_op jit(solution)/shard_map/psum | solution.py:43
  (816 shorter events, 535.9 us)
Async XLA Ops:
  7.2 102.5 %all-reduce.51.cloned.1.call-start = ((), (), s32[]{:S(2)}) async-start(), calls=%async_computation | async-start | bytes 2408448 | tf_op jit(solution)/shard_map/psum | solution.py:27
  28.6 168.4 %all-reduce.53.cloned.1.call-start = ((), (), s32[]{:S(2)}) async-start(), calls=%async_computation.1 | async-start | bytes 2408448 | tf_op jit(solution)/shard_map/psum | solution.py:27
  116.2 168.3 %all-reduce.55.cloned.1.call-start = ((), (), s32[]{:S(2)}) async-start(), calls=%async_computation.2 | async-start | bytes 2408448 | tf_op jit(solution)/shard_map/psum | solution.py:27
  203.6 168.3 %all-reduce.57.cloned.1.call-start = ((), (), s32[]{:S(2)}) async-start(), calls=%async_computation.3 | async-start | bytes 2408448 | tf_op jit(solution)/shard_map/psum | solution.py:27
  291.0 168.4 %all-reduce.59.cloned.1.call-start = ((), (), s32[]{:S(2)}) async-start(), calls=%async_computation.4 | async-start | bytes 2408448 | tf_op jit(solution)/shard_map/psum | solution.py:27
  378.5 168.3 %all-reduce.61.cloned.1.call-start = ((), (), s32[]{:S(2)}) async-start(), calls=%async_computation.5 | async-start | bytes 2408448 | tf_op jit(solution)/shard_map/psum | solution.py:27
  465.9 168.3 %all-reduce.63.cloned.1.call-start = ((), (), s32[]{:S(2)}) async-start(), calls=%async_computation.6 | async-start | bytes 2408448 | tf_op jit(solution)/shard_map/psum | solution.py:27
  553.4 168.3 %all-reduce.65.cloned.1.call-start = ((), (), s32[]{:S(2)}) async-start(), calls=%async_computation.7 | async-start | bytes 2408448 | tf_op jit(solution)/shard_map/psum | solution.py:27
  640.8 168.3 %all-reduce.67.cloned.1.call-start = ((), (), s32[]{:S(2)}) async-start(), calls=%async_computation.8 | async-start | bytes 2408448 | tf_op jit(solution)/shard_map/psum | solution.py:27
  728.2 168.3 %all-reduce.69.cloned.1.call-start = ((), (), s32[]{:S(2)}) async-start(), calls=%async_computation.9 | async-start | bytes 2408448 | tf_op jit(solution)/shard_map/psum | solution.py:27
  815.6 168.3 %all-reduce.71.cloned.1.call-start = ((), (), s32[]{:S(2)}) async-start(), calls=%async_computation.10 | async-start | bytes 2408448 | tf_op jit(solution)/shard_map/psum | solution.py:27
  903.1 168.1 %all-reduce.73.cloned.1.call-start = ((), (), s32[]{:S(2)}) async-start(), calls=%async_computation.11 | async-start | bytes 2408448 | tf_op jit(solution)/shard_map/psum | solution.py:27
  990.3 169.2 %all-reduce.75.cloned.1.call-start = ((), (), s32[]{:S(2)}) async-start(), calls=%async_computation.12 | async-start | bytes 2408448 | tf_op jit(solution)/shard_map/psum | solution.py:42
  1078.5 169.2 %all-reduce.77.cloned.1.call-start = ((), (), s32[]{:S(2)}) async-start(), calls=%async_computation.13 | async-start | bytes 2408448 | tf_op jit(solution)/shard_map/psum | solution.py:42
  1166.8 169.5 %all-reduce.79.cloned.1.call-start = ((), (), s32[]{:S(2)}) async-start(), calls=%async_computation.14 | async-start | bytes 2408448 | tf_op jit(solution)/shard_map/psum | solution.py:42
  1255.5 169.6 %all-reduce.81.cloned.1.call-start = ((), (), s32[]{:S(2)}) async-start(), calls=%async_computation.15 | async-start | bytes 2408448 | tf_op jit(solution)/shard_map/psum | solution.py:42
  1344.2 169.6 %all-reduce.83.cloned.1.call-start = ((), (), s32[]{:S(2)}) async-start(), calls=%async_computation.16 | async-start | bytes 2408448 | tf_op jit(solution)/shard_map/psum | solution.py:42
  1432.9 169.6 %all-reduce.85.cloned.1.call-start = ((), (), s32[]{:S(2)}) async-start(), calls=%async_computation.17 | async-start | bytes 2408448 | tf_op jit(solution)/shard_map/psum | solution.py:42
  1521.7 169.5 %all-reduce.87.cloned.1.call-start = ((), (), s32[]{:S(2)}) async-start(), calls=%async_computation.18 | async-start | bytes 2408448 | tf_op jit(solution)/shard_map/psum | solution.py:42
  1610.3 169.3 %all-reduce.89.cloned.1.call-start = ((), (), s32[]{:S(2)}) async-start(), calls=%async_computation.19 | async-start | bytes 2408448 | tf_op jit(solution)/shard_map/psum | solution.py:42
  1698.7 169.7 %all-reduce.91.cloned.1.call-start = ((), (), s32[]{:S(2)}) async-start(), calls=%async_computation.20 | async-start | bytes 2408448 | tf_op jit(solution)/shard_map/psum | solution.py:42
  1787.5 169.6 %all-reduce.93.cloned.1.call-start = ((), (), s32[]{:S(2)}) async-start(), calls=%async_computation.21 | async-start | bytes 2408448 | tf_op jit(solution)/shard_map/psum | solution.py:42
  1876.2 169.2 %all-reduce.95.cloned.1.call-start = ((), (), s32[]{:S(2)}) async-start(), calls=%async_computation.22 | async-start | bytes 2408448 | tf_op jit(solution)/shard_map/psum | solution.py:42
  1964.7 563.1 %all-reduce.145.cloned.1.call-start = ((), (), s32[]{:S(2)}) async-start(), calls=%async_computation.47 | async-start | bytes 56623104 | tf_op jit(solution)/shard_map/psum | solution.py:43
  2053.1 631.4 %all-reduce.97.cloned.1.call-start = ((), (), s32[]{:S(2)}) async-start(), calls=%async_computation.23 | async-start | bytes 2408448 | tf_op jit(solution)/shard_map/psum | solution.py:27
  2599.5 170.3 %all-reduce.99.cloned.1.call-start = ((), (), s32[]{:S(2)}) async-start(), calls=%async_computation.24 | async-start | bytes 2408448 | tf_op jit(solution)/shard_map/psum | solution.py:27
  2688.9 167.6 %all-reduce.101.cloned.1.call-start = ((), (), s32[]{:S(2)}) async-start(), calls=%async_computation.25 | async-start | bytes 2408448 | tf_op jit(solution)/shard_map/psum | solution.py:27
  2775.5 166.3 %all-reduce.103.cloned.1.call-start = ((), (), s32[]{:S(2)}) async-start(), calls=%async_computation.26 | async-start | bytes 2408448 | tf_op jit(solution)/shard_map/psum | solution.py:27
  2860.8 167.6 %all-reduce.105.cloned.1.call-start = ((), (), s32[]{:S(2)}) async-start(), calls=%async_computation.27 | async-start | bytes 2408448 | tf_op jit(solution)/shard_map/psum | solution.py:27
  2947.5 167.5 %all-reduce.107.cloned.1.call-start = ((), (), s32[]{:S(2)}) async-start(), calls=%async_computation.28 | async-start | bytes 2408448 | tf_op jit(solution)/shard_map/psum | solution.py:27
  3034.1 167.5 %all-reduce.109.cloned.1.call-start = ((), (), s32[]{:S(2)}) async-start(), calls=%async_computation.29 | async-start | bytes 2408448 | tf_op jit(solution)/shard_map/psum | solution.py:27
  3120.7 167.5 %all-reduce.111.cloned.1.call-start = ((), (), s32[]{:S(2)}) async-start(), calls=%async_computation.30 | async-start | bytes 2408448 | tf_op jit(solution)/shard_map/psum | solution.py:27
  3207.2 166.3 %all-reduce.113.cloned.1.call-start = ((), (), s32[]{:S(2)}) async-start(), calls=%async_computation.31 | async-start | bytes 2408448 | tf_op jit(solution)/shard_map/psum | solution.py:27
  3292.7 167.3 %all-reduce.115.cloned.1.call-start = ((), (), s32[]{:S(2)}) async-start(), calls=%async_computation.32 | async-start | bytes 2408448 | tf_op jit(solution)/shard_map/psum | solution.py:27
  3379.1 167.5 %all-reduce.117.cloned.1.call-start = ((), (), s32[]{:S(2)}) async-start(), calls=%async_computation.33 | async-start | bytes 2408448 | tf_op jit(solution)/shard_map/psum | solution.py:27
  3465.7 167.0 %all-reduce.119.cloned.1.call-start = ((), (), s32[]{:S(2)}) async-start(), calls=%async_computation.34 | async-start | bytes 2408448 | tf_op jit(solution)/shard_map/psum | solution.py:27
  3551.8 167.7 %all-reduce.121.cloned.1.call-start = ((), (), s32[]{:S(2)}) async-start(), calls=%async_computation.35 | async-start | bytes 2408448 | tf_op jit(solution)/shard_map/psum | solution.py:42
  3638.7 166.7 %all-reduce.123.cloned.1.call-start = ((), (), s32[]{:S(2)}) async-start(), calls=%async_computation.36 | async-start | bytes 2408448 | tf_op jit(solution)/shard_map/psum | solution.py:42
  3724.6 168.3 %all-reduce.125.cloned.1.call-start = ((), (), s32[]{:S(2)}) async-start(), calls=%async_computation.37 | async-start | bytes 2408448 | tf_op jit(solution)/shard_map/psum | solution.py:42
  3812.0 168.2 %all-reduce.127.cloned.1.call-start = ((), (), s32[]{:S(2)}) async-start(), calls=%async_computation.38 | async-start | bytes 2408448 | tf_op jit(solution)/shard_map/psum | solution.py:42
  3899.3 167.8 %all-reduce.129.cloned.1.call-start = ((), (), s32[]{:S(2)}) async-start(), calls=%async_computation.39 | async-start | bytes 2408448 | tf_op jit(solution)/shard_map/psum | solution.py:42
  3986.3 166.6 %all-reduce.131.cloned.1.call-start = ((), (), s32[]{:S(2)}) async-start(), calls=%async_computation.40 | async-start | bytes 2408448 | tf_op jit(solution)/shard_map/psum | solution.py:42
  4072.0 167.0 %all-reduce.133.cloned.1.call-start = ((), (), s32[]{:S(2)}) async-start(), calls=%async_computation.41 | async-start | bytes 2408448 | tf_op jit(solution)/shard_map/psum | solution.py:42
  4158.2 166.8 %all-reduce.135.cloned.1.call-start = ((), (), s32[]{:S(2)}) async-start(), calls=%async_computation.42 | async-start | bytes 2408448 | tf_op jit(solution)/shard_map/psum | solution.py:42
  4244.1 166.7 %all-reduce.137.cloned.1.call-start = ((), (), s32[]{:S(2)}) async-start(), calls=%async_computation.43 | async-start | bytes 2408448 | tf_op jit(solution)/shard_map/psum | solution.py:42
  4329.9 167.0 %all-reduce.139.cloned.1.call-start = ((), (), s32[]{:S(2)}) async-start(), calls=%async_computation.44 | async-start | bytes 2408448 | tf_op jit(solution)/shard_map/psum | solution.py:42
  4416.0 166.5 %all-reduce.141.cloned.1.call-start = ((), (), s32[]{:S(2)}) async-start(), calls=%async_computation.45 | async-start | bytes 2408448 | tf_op jit(solution)/shard_map/psum | solution.py:42
  4501.4 562.8 %all-reduce.143.cloned.1.call-start = ((), (), s32[]{:S(2)}) async-start(), calls=%async_computation.46 | async-start | bytes 56623104 | tf_op jit(solution)/shard_map/psum | solution.py:43
  (242 other events, 3879.0 us)
Sparse Core Ops, SparseCore 0:
  28.7 80.8 all-reduce.50
  116.3 80.6 all-reduce.52
  203.7 80.7 all-reduce.54
  291.1 80.7 all-reduce.56
  378.6 80.7 all-reduce.58
  466.1 80.6 all-reduce.60
  553.5 80.7 all-reduce.62
  640.9 80.6 all-reduce.64
  728.3 80.6 all-reduce.66
  815.8 80.6 all-reduce.68
  903.2 80.6 all-reduce.70
  990.4 80.6 all-reduce.72
  1078.6 80.7 all-reduce.74
  1166.9 80.6 all-reduce.76
  1255.6 80.6 all-reduce.78
  1344.3 80.7 all-reduce.80
  1433.0 80.7 all-reduce.82
  1521.8 80.7 all-reduce.84
  1610.4 80.6 all-reduce.86
  1698.8 80.6 all-reduce.88
  1787.7 80.6 all-reduce.90
  1876.4 80.7 all-reduce.92
  1964.8 80.6 all-reduce.94
  2053.2 474.4 all-reduce.144
  2599.6 84.8 all-reduce.96
  2689.0 80.7 all-reduce.98
  2775.6 80.7 all-reduce.100
  2860.9 80.7 all-reduce.102
  2947.7 80.7 all-reduce.104
  3034.2 80.7 all-reduce.106
  3120.8 80.7 all-reduce.108
  3207.3 80.8 all-reduce.110
  3292.8 80.6 all-reduce.112
  3379.3 80.6 all-reduce.114
  3465.8 80.7 all-reduce.116
  3551.9 80.7 all-reduce.118
  3638.8 80.6 all-reduce.120
  3724.7 80.6 all-reduce.122
  3812.1 80.6 all-reduce.124
  3899.4 80.7 all-reduce.126
  3986.4 80.6 all-reduce.128
  4072.1 80.7 all-reduce.130
  4158.3 80.5 all-reduce.132
  4244.2 80.7 all-reduce.134
  4330.0 80.7 all-reduce.136
  4416.1 80.6 all-reduce.138
  4501.6 80.8 all-reduce.140
  4589.8 474.4 all-reduce.142
where the time goes:
time: 5140 us; the launch traced here: 5130 us
  waiting for transfers between devices  4560 us (89%)
  matrix products  276 us (5%)
  other arithmetic  155 us (3%)
  local copies, waits for them, and re-layouts  79.6 us (2%)
    psum x24, waiting for transfers between devices, train_pass(): lax.psum(mix_part, 'model')  1920 us
    psum x22, waiting for transfers between devices, train_pass(): grad_h = grad_h + lax.psum(back_part, 'model')  1690 us
    psum x2, waiting for transfers between devices, train_pass(): lax.psum((g_in_loc.astype(jnp.float32), g_out_loc.astype(jnp.float32)), '...  941 us
  transfers between devices with their start and end apart: 48, of which 48 were waited for; matrix products, arithmetic and copies ran while one was open for 2% of the time, Pallas kernels for 0%

commit v1 on v0

v1 whole, which is shorter than its diff:
```python
import functools
import math

import jax
import jax.numpy as jnp
from jax import lax
from jax.experimental import pallas as pl
from jax.experimental.pallas import tpu as pltpu
from jax.sharding import PartitionSpec as P

MESH = pl.DeviceIdType.MESH
RHO_SCALE = 0.5
ETA = 1.0
HALF = 6
MB_IMAGES = 2
VMEM_LIMIT = 67043328
NN = (((1,), (0,)), ((), ()))
NT = (((1,), (1,)), ((), ()))
TN = (((0,), (0,)), ((), ()))
C0 = math.sqrt(2.0 / math.pi)
C1 = 0.044715


def dot(lhs, rhs, dims):
    return lax.dot_general(lhs, rhs, dims, preferred_element_type=jnp.float32)


def chip_of(pos):
    return 2 * (pos - 1) + 3 * lax.div(5 - pos, 5) - lax.div(pos, 5)


def static_chip(pos):
    return [1, 0, 2, 4, 6, 7][pos]


def locate():
    m = lax.axis_index("model")
    d = lax.axis_index("data")
    x, core = lax.div(d, 2), lax.rem(d, 2)
    z, y = lax.div(m, 2), lax.rem(m, 2)
    pos = (1 - y) * (z + 1) + y * 5 * lax.div(z, 3)
    idle = y * (1 - lax.div(z, 3)) * jnp.minimum(z, 1)
    stage = (1 - x) * pos + x * (11 - pos)
    return m, x, core, stage, idle == 0


def stage_device(stage, core):
    plane = lax.div(stage, HALF)
    pos = (1 - plane) * stage + plane * (11 - stage)
    return chip_of(pos), plane * 2 + core


def gather_kernel(win, wout, xin, yin, a_own, c_own, x_oth, y_oth, w_send, w_recv, loc_sem, xy_send, xy_recv):
    m, x, core, stage, active = locate()
    width = win.shape[2]
    mine = x * 2 + core
    partner = (1 - x) * 2 + core
    barrier = pltpu.get_barrier_semaphore()
    for step in range(1, 8):
        pl.semaphore_signal(barrier, inc=1, device_id=(lax.rem(m + step, 8), mine), device_id_type=MESH)
    pl.semaphore_signal(barrier, inc=1, device_id=(m, partner), device_id_type=MESH)
    pl.semaphore_wait(barrier, 8)

    xy = [
        pltpu.make_async_remote_copy(src, dst, xy_send.at[i], xy_recv.at[i], device_id=(m, partner), device_id_type=MESH)
        for i, (src, dst) in enumerate(((xin, x_oth), (yin, y_oth)))
    ]
    for copy in xy:
        copy.start()

    cols = pl.ds(pl.multiple_of(m * width, width), width)

    def ends(kind, layer, sl):
        if kind == 0:
            return win.at[layer], a_own.at[:, sl]
        return wout.at[layer], c_own.at[sl, :]

    for kind in (0, 1):
        @pl.when(core == kind)
        def _(kind=kind):
            for pos in range(HALF):
                dest = static_chip(pos)
                layer = (1 - x) * pos + x * (11 - pos)
                src, dst = ends(kind, layer, cols)

                @pl.when(m != dest)
                def _():
                    pltpu.make_async_remote_copy(src, dst, w_send.at[pos], w_recv.at[m], device_id=(dest, mine), device_id_type=MESH).start()

                @pl.when(m == dest)
                def _():
                    pltpu.make_async_copy(src, dst, loc_sem).start()

            for pos in range(HALF):
                dest = static_chip(pos)
                layer = (1 - x) * pos + x * (11 - pos)
                src, dst = ends(kind, layer, cols)

                @pl.when(m != dest)
                def _():
                    pltpu.make_async_remote_copy(src, dst, w_send.at[pos], w_recv.at[m], device_id=(dest, mine), device_id_type=MESH).wait_send()

                @pl.when(m == dest)
                def _():
                    pltpu.make_async_copy(src, dst, loc_sem).wait()

            @pl.when(active)
            def _():
                for peer in range(8):
                    src, dst = ends(kind, 0, pl.ds(peer * width, width))

                    @pl.when(m != peer)
                    def _():
                        pltpu.make_async_remote_copy(src, dst, w_send.at[0], w_recv.at[peer], device_id=(m, mine), device_id_type=MESH).wait_recv()

    for copy in xy:
        copy.wait()


def pass_kernel(cfg, a_in, c_in, x_ref, y_ref, ga_ref, gc_ref, ra_ref, rc_ref, loss_ref,
                a, c, hbuf, hout, zbuf, ubuf, ebuf, eout, ebb,
                w_send, w_recv, w_loc, g_send, g_recv, hs, hr, es, er):
    rows, per_shard, n_mb, res_scale = cfg
    m, x, core, stage, active = locate()
    width = x_ref.shape[1]
    hidden = a.shape[1]
    quarter = hidden // 4
    mine = x * 2 + core
    twin = x * 2 + (1 - core)
    prev_dev = stage_device(jnp.maximum(stage - 1, 0), core)
    next_dev = stage_device(jnp.minimum(stage + 1, 11), core)
    first = stage == 0
    last = stage == 11

    def block(mb):
        return pl.ds(pl.multiple_of(mb * rows, rows), rows)

    def h_copy(mb):
        return pltpu.make_async_remote_copy(hout.at[block(mb), :], hbuf.at[block(mb), :], hs.at[mb], hr.at[mb], device_id=next_dev, device_id_type=MESH)

    def e_copy(mb):
        return pltpu.make_async_remote_copy(eout.at[block(mb), :], ebuf.at[block(mb), :], es.at[mb], er.at[mb], device_id=prev_dev, device_id_type=MESH)

    def forward(mb):
        h = hbuf[block(mb), :]
        mix = None
        for q in range(4):
            sl = slice(q * quarter, (q + 1) * quarter)
            z = dot(h, a[:, sl], NN).astype(jnp.bfloat16)
            zf = z.astype(jnp.float32)
            u = (zf * (0.5 * (1.0 + jnp.tanh(C0 * (zf + C1 * (zf * zf * zf)))))).astype(jnp.bfloat16)
            zbuf[block(mb), sl] = z
            ubuf[block(mb), sl] = u
            part = dot(u, c[sl, :], NN)
            mix = part if mix is None else mix + part
        return (h.astype(jnp.float32) + mix).astype(jnp.bfloat16)

    def backward(mb, need_back):
        e = ebuf[block(mb), :]
        eb = e.astype(jnp.bfloat16)
        ebb[block(mb), :] = eb
        back = None
        for q in range(4):
            sl = slice(q * quarter, (q + 1) * quarter)
            du = dot(eb, c[sl, :], NT)
            zf = zbuf[block(mb), sl].astype(jnp.float32)
            z2 = zf * zf
            t = jnp.tanh(C0 * (zf + C1 * (z2 * zf)))
            slope = 0.5 * (1.0 + t) + (0.5 * zf) * ((1.0 - t * t) * (C0 + (3.0 * C0 * C1) * z2))
            dz = (slope * du).astype(jnp.bfloat16)
            zbuf[block(mb), sl] = dz
            if need_back:
                part = dot(dz, a[:, sl], NT)
                back = part if back is None else back + part
        if need_back:
            eout[block(mb), :] = e + back

    shard_rows = per_shard * rows

    def grad_piece(shard, q):
        span = pl.ds(shard * shard_rows, shard_rows)
        sl = slice(q * quarter, (q + 1) * quarter)
        gc = dot(ubuf[span, sl], ebb[span, :], TN).astype(jnp.bfloat16).astype(jnp.float32)
        ga = dot(hbuf[span, :], zbuf[span, sl], TN).astype(jnp.bfloat16).astype(jnp.float32)
        if shard == 0:
            gc_ref[sl, :] = gc
            ga_ref[:, sl] = ga
        else:
            gc_ref[sl, :] = gc_ref[sl, :] + gc
            ga_ref[:, sl] = ga_ref[:, sl] + ga

    a_loc = pltpu.make_async_copy(a_in, a, w_loc)
    c_loc = pltpu.make_async_copy(c_in, c, w_loc)
    a_rem = pltpu.make_async_remote_copy(a_in, a, w_send, w_recv, device_id=(m, twin), device_id_type=MESH)
    c_rem = pltpu.make_async_remote_copy(c_in, c, w_send, w_recv, device_id=(m, twin), device_id_type=MESH)
    a_grad = pltpu.make_async_remote_copy(ga_ref, ra_ref, g_send, g_recv, device_id=(m, twin), device_id_type=MESH)
    c_grad = pltpu.make_async_remote_copy(gc_ref, rc_ref, g_send, g_recv, device_id=(m, twin), device_id_type=MESH)

    barrier = pltpu.get_barrier_semaphore()
    loss_ref[...] = jnp.zeros_like(loss_ref)

    @pl.when(active)
    def _():
        pl.semaphore_signal(barrier, inc=1, device_id=(m, twin), device_id_type=MESH)

        @pl.when(stage > 0)
        def _():
            pl.semaphore_signal(barrier, inc=1, device_id=prev_dev, device_id_type=MESH)

        @pl.when(stage < 11)
        def _():
            pl.semaphore_signal(barrier, inc=1, device_id=next_dev, device_id_type=MESH)

        pl.semaphore_wait(barrier, 3 - lax.div(11 - stage, 11) - lax.div(stage, 11))

        @pl.when(core == 0)
        def _():
            a_rem.start()
            a_loc.start()

        @pl.when(core == 1)
        def _():
            c_rem.start()
            c_loc.start()

        @pl.when(first)
        def _():
            hbuf[...] = x_ref[...]

        @pl.when(core == 0)
        def _():
            a_loc.wait()
            a_rem.wait_send()
            c_rem.wait_recv()

        @pl.when(core == 1)
        def _():
            c_loc.wait()
            c_rem.wait_send()
            a_rem.wait_recv()

        def forward_step(mb, carry):
            @pl.when(stage > 0)
            def _():
                h_copy(mb).wait_recv()

            new_h = forward(mb)

            @pl.when(stage < 11)
            def _():
                hout[block(mb), :] = new_h
                h_copy(mb).start()

            @pl.when(last)
            def _():
                res = new_h.astype(jnp.float32) - y_ref[block(mb), :].astype(jnp.float32)
                loss_ref[...] = loss_ref[...] + jnp.sum(res * res, axis=0, keepdims=True)
                ebuf[block(mb), :] = res / res_scale
                backward(mb, True)
                e_copy(mb).start()

            return carry

        lax.fori_loop(0, n_mb, forward_step, 0)

        for shard in range(2):
            def backward_step(mb, carry):
                @pl.when(stage < 11)
                def _():
                    e_copy(mb).wait_recv()
                    backward(mb, True)

                    @pl.when(stage > 0)
                    def _():
                        e_copy(mb).start()

                return carry

            if shard == 0:
                lax.fori_loop(0, per_shard, backward_step, 0)
            else:
                for j in range(4):
                    lo, hi = n_mb // 2 + per_shard * j // 4, n_mb // 2 + per_shard * (j + 1) // 4
                    lax.fori_loop(lo, hi, backward_step, 0)
                    grad_piece(0, j)
        for q in range(4):
            grad_piece(1, q)

        @pl.when(core == 0)
        def _():
            c_grad.start()

        @pl.when(core == 1)
        def _():
            a_grad.start()

        def drain(mb, carry):
            @pl.when(stage < 11)
            def _():
                h_copy(mb).wait_send()

            @pl.when(stage > 0)
            def _():
                e_copy(mb).wait_send()

            return carry

        lax.fori_loop(0, n_mb, drain, 0)

        @pl.when(core == 0)
        def _():
            c_grad.wait_send()
            a_grad.wait_recv()

        @pl.when(core == 1)
        def _():
            a_grad.wait_send()
            c_grad.wait_recv()


def scatter_kernel(ga, gc, gin, gout, s1, r1, s2, r2, s3, r3, loc_sem):
    m, x, core, stage, active = locate()
    width = gin.shape[2]
    mine = x * 2 + core
    across = (1 - x) * 2 + core
    twin = x * 2 + (1 - core)
    barrier = pltpu.get_barrier_semaphore()
    for step in range(1, 8):
        pl.semaphore_signal(barrier, inc=1, device_id=(lax.rem(m + step, 8), mine), device_id_type=MESH)
    for other in (across, twin):
        pl.semaphore_signal(barrier, inc=1, device_id=(m, other), device_id_type=MESH)
    pl.semaphore_wait(barrier, 9)

    def piece(kind, peer):
        return ga.at[:, pl.ds(peer * width, width)] if kind == 0 else gc.at[pl.ds(peer * width, width), :]

    for kind in (0, 1):
        @pl.when(core == kind)
        def _(kind=kind):
            dst = gin if kind == 0 else gout
            other_dst = gout if kind == 0 else gin

            def first_hop(peer, layer, slot):
                return pltpu.make_async_remote_copy(piece(kind, peer), dst.at[layer], s1.at[peer], r1.at[slot], device_id=(peer, mine), device_id_type=MESH)

            def cross(layer, slot):
                return pltpu.make_async_remote_copy(dst.at[layer], dst.at[layer], s2.at[slot], r2.at[slot], device_id=(m, across), device_id_type=MESH)

            def to_twin(layer):
                return pltpu.make_async_remote_copy(dst.at[layer], dst.at[layer], s3.at[layer], r3.at[layer], device_id=(m, twin), device_id_type=MESH)

            def from_twin(layer):
                return pltpu.make_async_remote_copy(other_dst.at[layer], other_dst.at[layer], s3.at[layer], r3.at[layer], device_id=(m, twin), device_id_type=MESH)

            @pl.when(active)
            def _():
                for peer in range(8):
                    @pl.when(m != peer)
                    def _():
                        first_hop(peer, stage, stage - x * HALF).start()

                    @pl.when(m == peer)
                    def _():
                        pltpu.make_async_copy(piece(kind, peer), dst.at[stage], loc_sem).start()

            for slot in range(HALF):
                layer = x * HALF + slot
                is_mine = jnp.logical_and(active, stage == layer)

                @pl.when(is_mine)
                def _():
                    pltpu.make_async_copy(piece(kind, 0), dst.at[stage], loc_sem).wait()

                @pl.when(jnp.logical_not(is_mine))
                def _():
                    first_hop(0, layer, slot).wait_recv()

                cross(layer, slot).start()
                to_twin(layer).start()
            for slot in range(HALF):
                layer = (1 - x) * HALF + slot
                cross(layer, slot).wait_recv()
                to_twin(layer).start()
            for layer in range(2 * HALF):
                from_twin(layer).wait_recv()

            @pl.when(active)
            def _():
                for peer in range(8):
                    @pl.when(m != peer)
                    def _():
                        first_hop(peer, stage, stage - x * HALF).wait_send()

            for slot in range(HALF):
                cross(x * HALF + slot, slot).wait_send()
            for layer in range(2 * HALF):
                to_twin(layer).wait_send()


def comm_params(ident):
    return pltpu.CompilerParams(collective_id=ident, has_side_effects=True, vmem_limit_bytes=VMEM_LIMIT)


def any_spec(count):
    return [pl.BlockSpec(memory_space=pl.ANY)] * count


def vmem_spec(count):
    return [pl.BlockSpec(memory_space=pltpu.VMEM)] * count


def gather_blocks(win, wout, xin, yin):
    layers, depth, width = win.shape
    hidden = width * 8
    shape = jax.ShapeDtypeStruct
    dma = pltpu.SemaphoreType.DMA
    return pl.pallas_call(
        gather_kernel,
        out_shape=[shape((depth, hidden), win.dtype), shape((hidden, depth), win.dtype), shape(xin.shape, xin.dtype), shape(yin.shape, yin.dtype)],
        in_specs=any_spec(4),
        out_specs=any_spec(4),
        scratch_shapes=[dma((HALF,)), dma((8,)), dma, dma((2,)), dma((2,))],
        compiler_params=pltpu.CompilerParams(collective_id=0, has_side_effects=True),
        name="gather_blocks",
    )(win, wout, xin, yin)


def run_pass(a_in, c_in, x_mb, y_mb, rows, per_shard, res_scale, ident):
    depth, hidden = a_in.shape
    total = x_mb.shape[0]
    n_mb = total // rows
    shape = jax.ShapeDtypeStruct
    dma = pltpu.SemaphoreType.DMA
    f32, bf16 = jnp.float32, jnp.bfloat16
    return pl.pallas_call(
        functools.partial(pass_kernel, (rows, per_shard, n_mb, res_scale)),
        out_shape=[shape((depth, hidden), f32), shape((hidden, depth), f32), shape((depth, hidden), f32), shape((hidden, depth), f32), shape((1, depth), f32)],
        in_specs=any_spec(2) + vmem_spec(2),
        out_specs=vmem_spec(2) + any_spec(2) + vmem_spec(1),
        scratch_shapes=[
            pltpu.VMEM((depth, hidden), bf16),
            pltpu.VMEM((hidden, depth), bf16),
            pltpu.VMEM((total, depth), bf16),
            pltpu.VMEM((total, depth), bf16),
            pltpu.VMEM((total, hidden), bf16),
            pltpu.VMEM((total, hidden), bf16),
            pltpu.VMEM((total, depth), f32),
            pltpu.VMEM((total, depth), f32),
            pltpu.VMEM((total, depth), bf16),
            dma, dma, dma, dma, dma,
            dma((n_mb,)), dma((n_mb,)), dma((n_mb,)), dma((n_mb,)),
        ],
        compiler_params=comm_params(ident),
        name="pipeline_pass",
    )(a_in, c_in, x_mb, y_mb)


def scatter_grads(ga, gc, layers):
    depth, hidden = ga.shape
    width = hidden // 8
    shape = jax.ShapeDtypeStruct
    dma = pltpu.SemaphoreType.DMA
    return pl.pallas_call(
        scatter_kernel,
        out_shape=[shape((layers, depth, width), ga.dtype), shape((layers, width, depth), ga.dtype)],
        in_specs=any_spec(2),
        out_specs=any_spec(2),
        scratch_shapes=[dma((8,)), dma((HALF,)), dma((HALF,)), dma((HALF,)), dma((2 * HALF,)), dma((2 * HALF,)), dma],
        compiler_params=pltpu.CompilerParams(collective_id=3, has_side_effects=True),
        name="scatter_grads",
    )(ga, gc)


def solution(mesh):
    act_spec = P("data", None, None)
    in_spec = P(None, None, "model")
    out_spec = P(None, "model", None)

    def sam_step(x_tokens, y_target, w_in, w_out):
        rho = RHO_SCALE * math.sqrt(x_tokens.shape[-1] / w_in.shape[-1])
        elem_total = x_tokens.size
        n_data = mesh.shape["data"]

        def local_step(x_blk, y_blk, win_loc, wout_loc):
            layers = win_loc.shape[0]
            images, seq, depth = x_blk.shape
            m, x, core, stage, active = locate()
            raw = MB_IMAGES * seq
            rows = (raw + 15) // 16 * 16
            per_shard = images // MB_IMAGES

            def flat(blk):
                mbs = blk.reshape(per_shard, raw, depth)
                return jnp.pad(mbs, ((0, 0), (0, rows - raw), (0, 0))).reshape(per_shard * rows, depth)

            x_own, y_own = flat(x_blk), flat(y_blk)
            a_own, c_own, x_oth, y_oth = gather_blocks(win_loc, wout_loc, x_own, y_own)

            def both(own, oth):
                return jnp.where(x == 0, jnp.concatenate([own, oth]), jnp.concatenate([oth, own]))

            x_mb, y_mb = both(x_own, x_oth), both(y_own, y_oth)
            res_scale = float(images * seq * depth)

            def mean_pass(a_w, c_w, ident):
                ga, gc, ra, rc, loss = run_pass(a_w, c_w, x_mb, y_mb, rows, per_shard, res_scale, ident)
                return (ga + ra) / n_data, (gc + rc) / n_data, loss

            g_a, g_c, _ = mean_pass(a_own.astype(jnp.bfloat16), c_own.astype(jnp.bfloat16), 1)
            sq_a = jnp.where(jnp.logical_and(active, core == 0), jnp.sum(g_a * g_a), 0.0)
            sq_c = jnp.where(jnp.logical_and(active, core == 1), jnp.sum(g_c * g_c), 0.0)
            step_scale = rho / jnp.sqrt(lax.psum(sq_a + sq_c, ("model", "data")))
            pert_a = (a_own + step_scale * g_a).astype(jnp.bfloat16)
            pert_c = (c_own + step_scale * g_c).astype(jnp.bfloat16)
            g2_a, g2_c, loss = mean_pass(pert_a, pert_c, 2)
            loss_here = jnp.where(jnp.logical_and(active, stage == 11), 0.5 * jnp.sum(loss), 0.0)
            loss_val = lax.psum(loss_here, ("model", "data")) / elem_total
            grad_in, grad_out = scatter_grads(g2_a, g2_c, layers)
            return win_loc - ETA * grad_in, wout_loc - ETA * grad_out, loss_val

        stepper = jax.shard_map(local_step, mesh=mesh, in_specs=(act_spec, act_spec, in_spec, out_spec), out_specs=(in_spec, out_spec, P()), check_vma=False)
        return stepper(x_tokens, y_target, w_in, w_out)

    return sam_step
```

time: 5140 us -> 1280 us (0.25)
  waiting for transfers between devices: 4560 us -> 0 us
  Pallas kernels: 0 us -> 938 us
  matrix products: 276 us -> 0 us
  blocking collectives: 20.2 us -> 207 us
  local copies, waits for them, and re-layouts: 79.6 us -> 7.23 us
    psum x48 -> x0, waiting for transfers between devices: 4560 us -> none  [the longest x24 1920 us: train_pass(): lax.psum(mix_part, 'model')]
    pallas_call x0 -> x4, Pallas kernels: none -> 938 us  [the longest x2 470 us: run_pass(): pl.pallas_call(functools.partial(pass_kernel, (rows, per_shard, n_mb, res...]
    dot_general x140 -> x0, matrix products: 276 us -> none  [the longest x24 55.9 us: train_pass(): jnp.dot(act_b, w_out_b[layer_idx], preferred_element_type=jnp.float32)]
    psum x2, blocking collectives: 20.2 us -> 207 us  [the longest x1 110 us: local_step(): loss_val = lax.psum(loss_here, ('model', 'data')) / elem_total]
    unnamed x487 -> x10, local copies, waits for them, and re-layouts: 76.7 us -> 5.2 us
  transfers between devices with their start and end apart: 48 -> 0, of which waited for: 48 -> 0; matrix products, arithmetic and copies ran while one was open for 2% -> 0% of each run, Pallas kernels for 0% -> 0%
where the time goes in v1:
time: 1280 us; the launch traced here: 1270 us
  Pallas kernels  938 us (73%)
  blocking collectives  207 us (16%)
  other arithmetic  115 us (9%)
    pallas_call x2, Pallas kernels, run_pass(): pl.pallas_call(functools.partial(pass_kernel, (rows, per_shard, n_mb, res...  470 us
    pallas_call x1, Pallas kernels, scatter_grads(): pl.pallas_call(scatter_kernel, out_shape=[shape((layers, depth, width), g...  312 us
    pallas_call x1, Pallas kernels, gather_blocks(): pl.pallas_call(gather_kernel, out_shape=[shape((depth, hidden), win.dtype...  156 us
    psum x1, blocking collectives, local_step(): loss_val = lax.psum(loss_here, ('model', 'data')) / elem_total  110 us
    psum x1, blocking collectives, local_step(): step_scale = rho / jnp.sqrt(lax.psum(sq_a + sq_c, ('model', 'data')))  97.6 us
    sub x2, other arithmetic, local_step(): return (win_loc - ETA * grad_in, wout_loc - ETA * grad_out, loss_val)  26.9 us

profile of v1, /device:TPU:31, one launch (start us, length us, event | category | flops | bytes accessed | tf_op | source)
XLA Modules:
  0.0 1272.5 jit_solution(529907595934267168)
XLA Ops:
  0.7 1.2 copy.7
  1.8 0.1 reshape.18
  2.0 0.9 pad.7
  2.9 1.2 copy.8
  4.1 0.1 reshape.20
  4.2 0.9 pad.8
  5.1 0.0 copy-start.2
  5.1 0.0 copy-start.3
  5.1 155.8 %gather_blocks.1 = (f32[768,3072]{1,0:T(8,128)}, f32[3072,768]{1,0:T(8,128)}, bf16[448,768]{1,0:T(8,128)(2,1)}, bf16[448,768]{1,0:T(8,128)(2,1)}) custom-call(f32[12,768,384]{2,1,0:T(8,128)} %win.1, f32[12,384,768]{2,1,0:T(8,128)} %wout.1, bf16[448,768]{1,0:T(8,128)(2,1)} %bitcast.2, bf16[448,768]{1,0:T(8,128)(2,1)} %bitcast.4), custom_call_target="tpu_custom_call" | custom-call | tf_op jit(solution)/shard_map/gather_blocks/pallas_call | solution.py:417
  160.9 0.0 copy-done.2
  160.9 0.0 copy-done.3
  160.9 0.0 copy-start
  160.9 3.3 maximum_select_fusion
  164.2 7.3 convert_element_type.15.a_in
  171.6 0.0 copy-done
  171.6 2.6 convert_element_type.16.c_in
  174.2 233.0 %pipeline_pass.2 = (f32[768,3072]{1,0:T(8,128)}, f32[3072,768]{1,0:T(8,128)}, f32[768,3072]{1,0:T(8,128)}, f32[3072,768]{1,0:T(8,128)}, f32[1,768]{1,0:T(1,128)}) custom-call(bf16[768,3072]{1,0:T(8,128)(2,1)} %convert_element_type.15.a_in, bf16[3072,768]{1,0:T(8,128)(2,1)} %convert_element_type.16.c_in, bf16[896,768]{1,0:T(8,128)(2,1)} %get-tuple-element.37.x_ref, ...), custom_call_target="tpu_custom_call" | custom-call | tf_op jit(solution)/shard_map/pipeline_pass/pallas_call | solution.py:435
  407.2 14.4 %multiply_reduce_fusion.1 = (f32[]{:T(128)}, f32[768,3072]{1,0:T(8,128)}) fusion(f32[768,3072]{1,0:T(8,128)} %get-tuple-element.22, f32[768,3072]{1,0:T(8,128)} %get-tuple-element.23), kind=kLoop, calls=%fused_computation.5 | loop fusion | flops 9437183 | bytes 28311556 | tf_op jit(solution)/shard_map/reduce_sum | solution.py:510
  422.2 13.1 %multiply_reduce_fusion = (f32[]{:T(128)}, f32[3072,768]{1,0:T(8,128)}) fusion(f32[3072,768]{1,0:T(8,128)} %get-tuple-element.24, f32[3072,768]{1,0:T(8,128)} %get-tuple-element.25), kind=kLoop, calls=%fused_computation.4 | loop fusion | flops 9437183 | bytes 28311556 | tf_op jit(solution)/shard_map/reduce_sum | solution.py:511
  436.0 97.6 %psum.14 = f32[]{:T(128)} all-reduce(f32[]{:T(128)S(6)} %add.40), channel_id=1, replica_groups=mesh['model'=8,'data'=4] {'model','data'}, use_global_device_ids=true, to_apply=%region_2.3 | all-reduce | flops 1 | bytes 8 | tf_op jit(solution)/shard_map/psum | solution.py:512
  534.3 10.9 add_convert_fusion.1.a_in
  545.2 9.9 add_convert_fusion.c_in
  555.1 236.9 %pipeline_pass.3 = (f32[768,3072]{1,0:T(8,128)}, f32[3072,768]{1,0:T(8,128)}, f32[768,3072]{1,0:T(8,128)}, f32[3072,768]{1,0:T(8,128)}, f32[1,768]{1,0:T(1,128)}) custom-call(bf16[768,3072]{1,0:T(8,128)(2,1)} %add_convert_fusion.1.a_in, bf16[3072,768]{1,0:T(8,128)(2,1)} %add_convert_fusion.c_in, bf16[896,768]{1,0:T(8,128)(2,1)} %get-tuple-element.37.x_ref, ...), custom_call_target="tpu_custom_call" | custom-call | tf_op jit(solution)/shard_map/pipeline_pass/pallas_call | solution.py:435
  792.1 1.3 reduce_sum.29
  794.0 109.5 %psum.15 = f32[]{:T(128)} all-reduce(f32[]{:T(128)S(6)} %select_n.27), channel_id=1, replica_groups=mesh['model'=8,'data'=4] {'model','data'}, use_global_device_ids=true, to_apply=%region_4.5 | all-reduce | flops 1 | bytes 8 | tf_op jit(solution)/shard_map/psum | solution.py:517
  904.2 13.3 %add_multiply_fusion.1.ga = f32[768,3072]{1,0:T(8,128)} fusion(f32[768,3072]{1,0:T(8,128)} %get-tuple-element.26, f32[768,3072]{1,0:T(8,128)} %get-tuple-element.27), kind=kLoop, calls=%fused_computation.1 | loop fusion | flops 4718592 | bytes 28311552 | tf_op jit(solution)/shard_map/div | solution.py:507
  917.5 11.4 add_multiply_fusion.gc
  928.9 312.5 %scatter_grads.1 = (f32[12,768,384]{2,1,0:T(8,128)}, f32[12,384,768]{2,1,0:T(8,128)}) custom-call(f32[768,3072]{1,0:T(8,128)} %add_multiply_fusion.1.ga, f32[3072,768]{1,0:T(8,128)} %add_multiply_fusion.gc), custom_call_target="tpu_custom_call" | custom-call | tf_op jit(solution)/shard_map/scatter_grads/pallas_call | solution.py:463
  1241.4 0.0 copy-start.1
  1241.4 15.4 %sub.19 = f32[12,768,384]{2,1,0:T(8,128)} subtract(f32[12,768,384]{2,1,0:T(8,128)} %win.1, f32[12,768,384]{2,1,0:T(8,128)} %get-tuple-element.30) | non-fusion elementwise | flops 3538944 | bytes 42467328 | tf_op jit(solution)/shard_map/sub | solution.py:519
  1256.8 2.8 copy-done.1
  1259.6 11.5 sub.20
Async XLA Ops:
  5.1 155.8 %copy-start.2 = (bf16[4,112,768]{2,1,0:T(8,128)(2,1)S(1)}, bf16[4,112,768]{2,1,0:T(8,128)(2,1)}, u32[]{:S(2)}) copy-start(bf16[4,112,768]{2,1,0:T(8,128)(2,1)} %pad.7) | copy-start | bytes 2064388
  5.1 155.8 %copy-start.3 = (bf16[4,112,768]{2,1,0:T(8,128)(2,1)S(1)}, bf16[4,112,768]{2,1,0:T(8,128)(2,1)}, u32[]{:S(2)}) copy-start(bf16[4,112,768]{2,1,0:T(8,128)(2,1)} %pad.8) | copy-start | bytes 2064388
  160.9 10.7 copy-start
  1241.4 18.2 %copy-start.1 = (f32[12,384,768]{2,1,0:T(8,128)S(1)}, f32[12,384,768]{2,1,0:T(8,128)}, u32[]{:S(2)}) copy-start(f32[12,384,768]{2,1,0:T(8,128)} %get-tuple-element.31) | copy-start | bytes 42467332

commit v2 on v0

v2 whole, which is shorter than its diff:
```python
import functools
import math

import jax
import jax.numpy as jnp
from jax import lax
from jax.experimental import pallas as pl
from jax.experimental.pallas import tpu as pltpu
from jax.sharding import PartitionSpec as P

MESH = pl.DeviceIdType.MESH
RHO_SCALE = 0.5
ETA = 1.0
HALF = 6
MB_IMAGES = 2
VMEM_LIMIT = 67043328
NN = (((1,), (0,)), ((), ()))
NT = (((1,), (1,)), ((), ()))
TN = (((0,), (0,)), ((), ()))
C0 = math.sqrt(2.0 / math.pi)
C1 = 0.044715
CHIPS = (1, 0, 2, 4, 6, 7)
STRIP = 128


def dot(lhs, rhs, dims):
    return lax.dot_general(lhs, rhs, dims, preferred_element_type=jnp.float32)


def chip_of(pos):
    return 2 * (pos - 1) + 3 * lax.div(5 - pos, 5) - lax.div(pos, 5)


def locate():
    m = lax.axis_index("model")
    d = lax.axis_index("data")
    x, core = lax.div(d, 2), lax.rem(d, 2)
    z, y = lax.div(m, 2), lax.rem(m, 2)
    pos = (1 - y) * (z + 1) + y * 5 * lax.div(z, 3)
    idle = y * (1 - lax.div(z, 3)) * jnp.minimum(z, 1)
    stage = (1 - x) * pos + x * (11 - pos)
    return m, x, core, stage, idle == 0


def stage_device(stage, core):
    plane = lax.div(stage, HALF)
    pos = (1 - plane) * stage + plane * (11 - stage)
    return chip_of(pos), plane * 2 + core


def step_kernel(cfg, win, wout, xin, yin,
                gin, gout, a_own, c_own, loss_out,
                a, c, ga, gc, rem, xbuf, ybuf, hbuf, hout, zbuf, ubuf, ebuf, eout, ebb,
                acc, nrm_send, nrm, loss_send,
                w_send, w_recv, w_loc, xy_send, xy_recv, xy_loc, stage_loc, t_send, t_recv, g_send, g_recv,
                hs, hr, es, er, stagger, n_send, n_recv, l_send, l_recv,
                s1, r1, s2, r2, s3, r3, s_loc):
    rows, per_shard, n_mb, res_scale, rho, n_data = cfg
    m, x, core, stage, active = locate()
    depth, hidden = a.shape
    width = hidden // 8
    quarter = hidden // 4
    strips = quarter // STRIP
    shard_rows = per_shard * rows
    mine = x * 2 + core
    across = (1 - x) * 2 + core
    twin = x * 2 + (1 - core)
    prev_dev = stage_device(jnp.maximum(stage - 1, 0), core)
    next_dev = stage_device(jnp.minimum(stage + 1, 11), core)
    last = stage == 11

    def remote(src, dst, send, recv, dev):
        return pltpu.make_async_remote_copy(src, dst, send, recv, device_id=dev, device_id_type=MESH)

    barrier = pltpu.get_barrier_semaphore()
    here = m * 4 + mine
    for step in range(1, 32):
        there = lax.rem(here + step, 32)
        pl.semaphore_signal(barrier, inc=1, device_id=(lax.div(there, 4), lax.rem(there, 4)), device_id_type=MESH)
    pl.semaphore_wait(barrier, 31)

    def weight_ends(kind, layer, shard):
        sl = pl.ds(pl.multiple_of(shard * width, width), width)
        return (win.at[layer], a_own.at[:, sl]) if kind == 0 else (wout.at[layer], c_own.at[sl, :])

    def weight_copy(kind, j, shard):
        layer = x * HALF + j
        src, dst = weight_ends(kind, layer, shard)
        dest = chip_of((1 - x) * j + x * (5 - j))
        return dest, remote(src, dst, w_send.at[j], w_recv.at[shard], (dest, mine)), pltpu.make_async_copy(src, dst, w_loc)

    for kind in (0, 1):
        @pl.when(core == kind)
        def _(kind=kind):
            for j in range(HALF):
                dest, far, near = weight_copy(kind, j, m)

                @pl.when(m != dest)
                def _():
                    far.start()

                @pl.when(m == dest)
                def _():
                    near.start()

    own_rows = pl.ds(pl.multiple_of(x * shard_rows, shard_rows), shard_rows)
    xy_far = [remote(src, dst.at[own_rows, :], xy_send.at[i], xy_recv.at[i], (m, across)) for i, (src, dst) in enumerate(((xin, xbuf), (yin, ybuf)))]
    xy_near = [pltpu.make_async_copy(src, dst.at[own_rows, :], xy_loc.at[i]) for i, (src, dst) in enumerate(((xin, xbuf), (yin, ybuf)))]
    for copy in xy_far + xy_near:
        copy.start()
    for copy in xy_near + xy_far:
        copy.wait()

    def piece(kind, ref_a, ref_c, q):
        sl = pl.ds(pl.multiple_of(q * quarter, quarter), quarter)
        return ref_a.at[:, sl] if kind == 0 else ref_c.at[sl, :]

    def strip(kind, ref_a, ref_c, q, i):
        cols = pl.ds(pl.multiple_of(q * quarter, quarter), quarter)
        if kind == 0:
            return ref_a, (pl.ds(pl.multiple_of(i * STRIP, STRIP), STRIP), cols)
        return ref_c, (pl.ds(pl.multiple_of(q * quarter + i * STRIP, STRIP), STRIP), slice(None))

    def strip_rows(i):
        return pl.ds(pl.multiple_of(i * STRIP, STRIP), STRIP)

    stagings = (ebuf, eout)

    def master_copy(kind, q):
        return pltpu.make_async_copy(piece(kind, a_own, c_own, q), stagings[q % 2].at[pl.ds(0, depth), :], stage_loc.at[q % 2])

    def twin_copy(kind, q):
        ref = piece(kind, a, c, q)
        return remote(ref, ref, t_send.at[q], t_recv.at[q], (m, twin))

    def grad_copy(kind, q):
        return remote(piece(kind, ga, gc, q), rem.at[q], g_send.at[q], g_recv.at[q], (m, twin))

    def load_weights(kind, scale):
        for q in range(4):
            if scale is None or q >= 2:
                master_copy(kind, q).start() if scale is not None else None
            if scale is None:
                for shard in (2 * q, 2 * q + 1):
                    far = remote(weight_ends(kind, 0, shard)[0], weight_ends(kind, 0, shard)[1], w_send.at[0], w_recv.at[shard], (m, mine))

                    @pl.when(m != shard)
                    def _():
                        far.wait_recv()

                    @pl.when(m == shard)
                    def _():
                        pltpu.make_async_copy(weight_ends(kind, 0, shard)[0], weight_ends(kind, 0, shard)[1], w_loc).wait()

                master_copy(kind, q).start()
            master_copy(kind, q).wait()

            def round_strip(i, carry):
                dst, where = strip(kind, a, c, q, i)
                value = stagings[q % 2][strip_rows(i), :]
                if scale is not None:
                    src, _ = strip(kind, ga, gc, q, i)
                    value = value + scale * src[where]
                dst[where] = value.astype(jnp.bfloat16)
                return carry

            lax.fori_loop(0, strips, round_strip, 0)
            twin_copy(kind, q).start()
        for q in range(4):
            twin_copy(kind, q).wait_send()
        for q in range(4):
            twin_copy(1 - kind, q).wait_recv()

    def block(mb):
        return pl.ds(pl.multiple_of(mb * rows, rows), rows)

    def h_copy(mb):
        return remote(hout.at[block(mb), :], hbuf.at[block(mb), :], hs.at[mb], hr.at[mb], next_dev)

    def e_copy(mb):
        return remote(eout.at[block(mb), :], ebuf.at[block(mb), :], es.at[mb], er.at[mb], prev_dev)

    def forward(mb):
        h = hbuf[block(mb), :]
        mix = None
        for q in range(4):
            sl = slice(q * quarter, (q + 1) * quarter)
            z = dot(h, a[:, sl], NN).astype(jnp.bfloat16)
            zf = z.astype(jnp.float32)
            u = (zf * (0.5 * (1.0 + jnp.tanh(C0 * (zf + C1 * (zf * zf * zf)))))).astype(jnp.bfloat16)
            zbuf[block(mb), sl] = z
            ubuf[block(mb), sl] = u
            part = dot(u, c[sl, :], NN)
            mix = part if mix is None else mix + part
        return (h.astype(jnp.float32) + mix).astype(jnp.bfloat16)

    def backward(mb):
        e = ebuf[block(mb), :]
        eb = e.astype(jnp.bfloat16)
        ebb[block(mb), :] = eb
        back = None
        for q in range(4):
            sl = slice(q * quarter, (q + 1) * quarter)
            du = dot(eb, c[sl, :], NT)
            zf = zbuf[block(mb), sl].astype(jnp.float32)
            z2 = zf * zf
            t = jnp.tanh(C0 * (zf + C1 * (z2 * zf)))
            slope = 0.5 * (1.0 + t) + (0.5 * zf) * ((1.0 - t * t) * (C0 + (3.0 * C0 * C1) * z2))
            dz = (slope * du).astype(jnp.bfloat16)
            zbuf[block(mb), sl] = dz
            part = dot(dz, a[:, sl], NT)
            back = part if back is None else back + part
        eout[block(mb), :] = e + back

    def grad_piece(shard, q):
        span = pl.ds(shard * shard_rows, shard_rows)
        sl = pl.ds(pl.multiple_of(q * quarter, quarter), quarter)
        d_out = dot(ubuf[span, sl], ebb[span, :], TN).astype(jnp.bfloat16).astype(jnp.float32)
        gc[sl, :] = d_out if shard == 0 else gc[sl, :] + d_out
        d_in = dot(hbuf[span, :], zbuf[span, sl], TN).astype(jnp.bfloat16).astype(jnp.float32)
        ga[:, sl] = d_in if shard == 0 else ga[:, sl] + d_in

    def on_core(fn):
        for kind in (0, 1):
            @pl.when(core == kind)
            def _(kind=kind):
                fn(kind)

    def run_pass(p, carry):
        acc[...] = jnp.zeros_like(acc)

        @pl.when(stage == 0)
        def _():
            hbuf[...] = xbuf[...]

            @pl.when(core == 1)
            def _():
                pl.semaphore_wait(stagger, 1)

        def forward_step(mb, carry):
            @pl.when(stage > 0)
            def _():
                h_copy(mb).wait_recv()

            new_h = forward(mb)

            @pl.when(stage < 11)
            def _():
                hout[block(mb), :] = new_h
                h_copy(mb).start()

            @pl.when(jnp.logical_and(stage == 0, jnp.logical_and(core == 0, mb == 0)))
            def _():
                pl.semaphore_signal(stagger, inc=1, device_id=(m, twin), device_id_type=MESH)

            @pl.when(last)
            def _():
                res = new_h.astype(jnp.float32) - ybuf[block(mb), :].astype(jnp.float32)
                acc[...] = acc[...] + jnp.sum(res * res, axis=0, keepdims=True)
                ebuf[block(mb), :] = res / res_scale
                backward(mb)
                e_copy(mb).start()

            return carry

        lax.fori_loop(0, n_mb, forward_step, 0)

        def fold(dst):
            total = acc[:, 0:128]
            for i in range(1, depth // 128):
                total = total + acc[:, i * 128:(i + 1) * 128]
            dst[...] = jnp.broadcast_to(total, dst.shape)

        @pl.when(jnp.logical_and(last, p == 1))
        def _():
            fold(loss_send)
            for step in range(32):
                pltpu_copy = remote(loss_send, loss_out.at[core], l_send.at[step], l_recv.at[core], (step // 4, step % 4))

                @pl.when(here != step)
                def _():
                    pltpu_copy.start()

            loss_out[core] = loss_send[...]
            for step in range(32):
                pltpu_copy = remote(loss_send, loss_out.at[core], l_send.at[step], l_recv.at[core], (step // 4, step % 4))

                @pl.when(here != step)
                def _():
                    pltpu_copy.wait_send()

        def backward_step(mb):
            @pl.when(stage < 11)
            def _():
                e_copy(mb).wait_recv()
                backward(mb)

                @pl.when(stage > 0)
                def _():
                    e_copy(mb).start()

        def first_shard(mb, carry):
            backward_step(mb)
            return carry

        def second_shard(mb, carry):
            backward_step(per_shard + mb)
            grad_piece(0, mb)
            return carry

        def tail_grads(q, carry):
            grad_piece(1, q)
            on_core(lambda kind: grad_copy(1 - kind, q).start())
            return carry

        lax.fori_loop(0, per_shard, first_shard, 0)
        lax.fori_loop(0, per_shard, second_shard, 0)
        lax.fori_loop(0, 4, tail_grads, 0)

        def drain(mb, carry):
            @pl.when(stage < 11)
            def _():
                h_copy(mb).wait_send()

            @pl.when(stage > 0)
            def _():
                e_copy(mb).wait_send()

            return carry

        lax.fori_loop(0, n_mb, drain, 0)

        def between(kind):
            for q in range(2):
                master_copy(kind, q).start()
            acc[...] = jnp.zeros_like(acc)

            def total_quarter(q, carry):
                grad_copy(kind, q).wait_recv()

                def total_strip(i, carry):
                    ref, where = strip(kind, ga, gc, q, i)
                    total = (ref[where] + rem[q, strip_rows(i), :]) / n_data
                    ref[where] = total
                    acc[...] = acc[...] + jnp.sum(total * total, axis=0, keepdims=True)
                    return carry

                return lax.fori_loop(0, strips, total_strip, carry)

            lax.fori_loop(0, 4, total_quarter, 0)
            fold(nrm_send)
            slot = stage * 2 + core

            def norm_copies():
                for s in range(12):
                    chip = CHIPS[s] if s < HALF else CHIPS[11 - s]
                    for k in range(2):
                        dev = (chip, (s // HALF) * 2 + k)
                        yield s * 2 + k, remote(nrm_send, nrm.at[slot], n_send.at[s * 2 + k], n_recv.at[slot], dev)

            for i, copy in norm_copies():
                @pl.when(slot != i)
                def _():
                    copy.start()

            nrm[slot] = nrm_send[...]
            for i, copy in norm_copies():
                @pl.when(slot != i)
                def _():
                    copy.wait_send()
                    remote(nrm_send, nrm.at[i], n_send.at[i], n_recv.at[i], (m, mine)).wait_recv()

            square = jnp.sum(jnp.sum(nrm[:, 0, :], axis=0, keepdims=True), axis=1, keepdims=True)
            for q in range(4):
                grad_copy(1 - kind, q).wait_send()
            load_weights(kind, rho / jnp.sqrt(square))

        @pl.when(p == 0)
        def _():
            on_core(between)

        return carry

    @pl.when(active)
    def _():
        on_core(lambda kind: load_weights(kind, None))
        lax.fori_loop(0, 2, run_pass, 0)

    def scatter(kind):
        dst = gin if kind == 0 else gout
        other_dst = gout if kind == 0 else gin

        def ends(peer):
            sl = pl.ds(pl.multiple_of(peer * width, width), width)
            return ga.at[:, sl] if kind == 0 else gc.at[sl, :]

        def first_hop(peer, layer, slot):
            return remote(ends(peer), dst.at[layer], s1.at[peer], r1.at[slot], (peer, mine))

        def cross(layer, slot):
            return remote(dst.at[layer], dst.at[layer], s2.at[slot], r2.at[slot], (m, across))

        def to_twin(layer):
            return remote(dst.at[layer], dst.at[layer], s3.at[layer], r3.at[layer], (m, twin))

        def from_twin(layer):
            return remote(other_dst.at[layer], other_dst.at[layer], s3.at[layer], r3.at[layer], (m, twin))

        @pl.when(active)
        def _():
            def send_quarter(q, carry):
                grad_copy(kind, q).wait_recv()

                def total_strip(i, carry):
                    ref, where = strip(kind, ga, gc, q, i)
                    ref[where] = (ref[where] + rem[q, strip_rows(i), :]) / n_data
                    return carry

                lax.fori_loop(0, strips, total_strip, 0)
                for k in range(2):
                    peer = 2 * q + k

                    @pl.when(m != peer)
                    def _():
                        first_hop(peer, stage, stage - x * HALF).start()

                    @pl.when(m == peer)
                    def _():
                        pltpu.make_async_copy(ends(peer), dst.at[stage], s_loc).start()

                return carry

            lax.fori_loop(0, 4, send_quarter, 0)

        for slot in reversed(range(HALF)):
            layer = x * HALF + slot
            is_mine = jnp.logical_and(active, stage == layer)

            @pl.when(is_mine)
            def _():
                pltpu.make_async_copy(ends(0), dst.at[layer], s_loc).wait()

            @pl.when(jnp.logical_not(is_mine))
            def _():
                first_hop(0, layer, slot).wait_recv()

            cross(layer, slot).start()
            to_twin(layer).start()
        for slot in reversed(range(HALF)):
            layer = (1 - x) * HALF + slot
            cross(layer, slot).wait_recv()
            to_twin(layer).start()
        for layer in range(2 * HALF):
            from_twin(layer).wait_recv()

        @pl.when(active)
        def _():
            for peer in range(8):
                @pl.when(m != peer)
                def _():
                    first_hop(peer, stage, stage - x * HALF).wait_send()

            for q in range(4):
                grad_copy(1 - kind, q).wait_send()

        for slot in range(HALF):
            cross(x * HALF + slot, slot).wait_send()
        for layer in range(2 * HALF):
            to_twin(layer).wait_send()

        for j in range(HALF):
            dest, far, _ = weight_copy(kind, j, m)

            @pl.when(m != dest)
            def _():
                far.wait_send()

    on_core(scatter)

    for k in range(2):
        @pl.when(jnp.logical_not(jnp.logical_and(active, jnp.logical_and(last, core == k))))
        def _():
            remote(loss_send, loss_out.at[k], l_send.at[0], l_recv.at[k], (m, mine)).wait_recv()


def run_step(win, wout, xin, yin, rows, per_shard, res_scale, rho, n_data):
    layers, depth, width = win.shape
    hidden = width * 8
    total = 2 * per_shard * rows
    n_mb = 2 * per_shard
    shape = jax.ShapeDtypeStruct
    dma = pltpu.SemaphoreType.DMA
    f32, bf16 = jnp.float32, jnp.bfloat16
    any_space = pl.BlockSpec(memory_space=pl.ANY)
    return pl.pallas_call(
        functools.partial(step_kernel, (rows, per_shard, n_mb, res_scale, rho, n_data)),
        out_shape=[shape(win.shape, f32), shape(wout.shape, f32), shape((depth, hidden), f32), shape((hidden, depth), f32), shape((2, 8, 128), f32)],
        in_specs=[any_space] * 4,
        out_specs=[any_space] * 4 + [pl.BlockSpec(memory_space=pltpu.VMEM)],
        scratch_shapes=[
            pltpu.VMEM((depth, hidden), bf16),
            pltpu.VMEM((hidden, depth), bf16),
            pltpu.VMEM((depth, hidden), f32),
            pltpu.VMEM((hidden, depth), f32),
            pltpu.VMEM((4, depth, hidden // 4), f32) if depth == hidden // 4 else pltpu.VMEM((4, depth, depth), f32),
            pltpu.VMEM((total, depth), bf16),
            pltpu.VMEM((total, depth), bf16),
            pltpu.VMEM((total, depth), bf16),
            pltpu.VMEM((total, depth), bf16),
            pltpu.VMEM((total, hidden), bf16),
            pltpu.VMEM((total, hidden), bf16),
            pltpu.VMEM((total, depth), f32),
            pltpu.VMEM((total, depth), f32),
            pltpu.VMEM((total, depth), bf16),
            pltpu.VMEM((1, depth), f32),
            pltpu.VMEM((8, 128), f32),
            pltpu.VMEM((24, 8, 128), f32),
            pltpu.VMEM((8, 128), f32),
            dma((HALF,)), dma((8,)), dma, dma((2,)), dma((2,)), dma((2,)), dma((2,)), dma((4,)), dma((4,)), dma((4,)), dma((4,)),
            dma((n_mb,)), dma((n_mb,)), dma((n_mb,)), dma((n_mb,)), pltpu.SemaphoreType.REGULAR,
            dma((24,)), dma((24,)), dma((32,)), dma((2,)),
            dma((8,)), dma((HALF,)), dma((HALF,)), dma((HALF,)), dma((2 * HALF,)), dma((2 * HALF,)), dma,
        ],
        compiler_params=pltpu.CompilerParams(collective_id=0, has_side_effects=True, vmem_limit_bytes=VMEM_LIMIT),
        name="sam_step",
    )(win, wout, xin, yin)


def solution(mesh):
    act_spec = P("data", None, None)
    in_spec = P(None, None, "model")
    out_spec = P(None, "model", None)

    def sam_step(x_tokens, y_target, w_in, w_out):
        rho = RHO_SCALE * math.sqrt(x_tokens.shape[-1] / w_in.shape[-1])
        elem_total = x_tokens.size
        n_data = mesh.shape["data"]

        def local_step(x_blk, y_blk, win_loc, wout_loc):
            images, seq, depth = x_blk.shape
            raw = MB_IMAGES * seq
            rows = (raw + 15) // 16 * 16
            per_shard = images // MB_IMAGES

            def flat(blk):
                mbs = blk.reshape(per_shard, raw, depth)
                return jnp.pad(mbs, ((0, 0), (0, rows - raw), (0, 0))).reshape(per_shard * rows, depth)

            res_scale = float(images * seq * depth)
            grad_in, grad_out, _, _, loss = run_step(win_loc, wout_loc, flat(x_blk), flat(y_blk), rows, per_shard, res_scale, rho, n_data)
            loss_val = 0.5 * jnp.sum(loss[:, 0, :]) / elem_total
            return win_loc - ETA * grad_in, wout_loc - ETA * grad_out, loss_val

        stepper = jax.shard_map(local_step, mesh=mesh, in_specs=(act_spec, act_spec, in_spec, out_spec), out_specs=(in_spec, out_spec, P()), check_vma=False)
        return stepper(x_tokens, y_target, w_in, w_out)

    return sam_step
```

time: 5140 us -> 1170 us (0.23)
  waiting for transfers between devices: 4560 us -> 0 us
  Pallas kernels: 0 us -> 1130 us
  matrix products: 276 us -> 0 us
  other arithmetic: 155 us -> 28.2 us
  local copies, waits for them, and re-layouts: 79.6 us -> 7.22 us
    psum x48 -> x0, waiting for transfers between devices: 4560 us -> none  [the longest x24 1920 us: train_pass(): lax.psum(mix_part, 'model')]
    pallas_call x0 -> x1, Pallas kernels: none -> 1130 us  [run_step(): pl.pallas_call(functools.partial(step_kernel, (rows, per_shard, n_mb, res...]
    dot_general x140 -> x0, matrix products: 276 us -> none  [the longest x24 55.9 us: train_pass(): jnp.dot(act_b, w_out_b[layer_idx], preferred_element_type=jnp.float32)]
    unnamed x487 -> x4, local copies, waits for them, and re-layouts: 76.7 us -> 5.19 us
    convert_element_type x30 -> x0, other arithmetic: 65.9 us -> none  [the longest x22 31.2 us: train_pass(): (hidden.astype(jnp.float32) + lax.psum(mix_part, 'model')).astype(jnp.bfl...]
  transfers between devices with their start and end apart: 48 -> 0, of which waited for: 48 -> 0; matrix products, arithmetic and copies ran while one was open for 2% -> 0% of each run, Pallas kernels for 0% -> 0%
where the time goes in v2:
time: 1170 us
  Pallas kernels  1130 us (97%)
  other arithmetic  28.2 us (2%)
    pallas_call x1, Pallas kernels, run_step(): pl.pallas_call(functools.partial(step_kernel, (rows, per_shard, n_mb, res...  1130 us
    sub x2, other arithmetic, local_step(): return (win_loc - ETA * grad_in, wout_loc - ETA * grad_out, loss_val)  26.9 us

profile of v2, /device:TPU:31, one launch (start us, length us, event | category | flops | bytes accessed | tf_op | source)
XLA Modules:
  0.0 1169.3 jit_solution(16028278801256328454)
XLA Ops:
  0.6 1.2 copy.7
  1.8 0.1 reshape.18
  1.9 0.9 pad.7
  2.8 1.2 copy.8
  4.0 0.1 reshape.20
  4.1 0.9 pad.8
  5.0 1131.4 %sam_step.1 = (f32[12,768,384]{2,1,0:T(8,128)}, f32[12,384,768]{2,1,0:T(8,128)}, f32[768,3072]{1,0:T(8,128)}, f32[3072,768]{1,0:T(8,128)}, f32[2,8,128]{2,1,0:T(8,128)}) custom-call(f32[12,768,384]{2,1,0:T(8,128)} %win.1, f32[12,384,768]{2,1,0:T(8,128)} %wout.1, bf16[448,768]{1,0:T(8,128)(2,1)} %bitcast.2, bf16[448,768]{1,0:T(8,128)(2,1)} %bitcast.3), custom_call_target="tpu_custom_call" | custom-call | tf_op jit(solution)/shard_map/sam_step/pallas_call | solution.py:495
  1136.4 1.3 slice_reduce_fusion
  1138.4 0.0 copy-start
  1138.4 15.4 %sub.6 = f32[12,768,384]{2,1,0:T(8,128)} subtract(f32[12,768,384]{2,1,0:T(8,128)} %win.1, f32[12,768,384]{2,1,0:T(8,128)} %get-tuple-element.6) | non-fusion elementwise | flops 3538944 | bytes 42467328 | tf_op jit(solution)/shard_map/sub | solution.py:552
  1153.8 2.8 copy-done
  1156.6 11.5 sub.7
Async XLA Ops:
  1138.4 18.2 %copy-start = (f32[12,384,768]{2,1,0:T(8,128)S(1)}, f32[12,384,768]{2,1,0:T(8,128)}, u32[]{:S(2)}) copy-start(f32[12,384,768]{2,1,0:T(8,128)} %get-tuple-element.7) | copy-start | bytes 42467332

commit v3 on v2

--- a/solution.py
+++ b/solution.py
@@ -12,7 +12,7 @@
 RHO_SCALE = 0.5
 ETA = 1.0
 HALF = 6
-MB_IMAGES = 2
+MB_IMAGES = 1
 VMEM_LIMIT = 67043328
 NN = (((1,), (0,)), ((), ()))
 NT = (((1,), (1,)), ((), ()))
@@ -49,13 +49,13 @@
 
 
 def step_kernel(cfg, win, wout, xin, yin,
-                gin, gout, a_own, c_own, loss_out,
-                a, c, ga, gc, rem, xbuf, ybuf, hbuf, hout, zbuf, ubuf, ebuf, eout, ebb,
+                gin, gout, a_own, c_own, x_all, loss_out,
+                a, c, ga, gc, rem, ybuf, hbuf, hout, zbuf, ubuf, ebuf, ebb,
                 acc, nrm_send, nrm, loss_send,
                 w_send, w_recv, w_loc, xy_send, xy_recv, xy_loc, stage_loc, t_send, t_recv, g_send, g_recv,
                 hs, hr, es, er, stagger, n_send, n_recv, l_send, l_recv,
                 s1, r1, s2, r2, s3, r3, s_loc):
-    rows, per_shard, n_mb, res_scale, rho, n_data = cfg
+    rows, sent, per_shard, n_mb, res_scale, rho, n_data = cfg
     m, x, core, stage, active = locate()
     depth, hidden = a.shape
     width = hidden // 8
@@ -104,8 +104,8 @@
                     near.start()
 
     own_rows = pl.ds(pl.multiple_of(x * shard_rows, shard_rows), shard_rows)
-    xy_far = [remote(src, dst.at[own_rows, :], xy_send.at[i], xy_recv.at[i], (m, across)) for i, (src, dst) in enumerate(((xin, xbuf), (yin, ybuf)))]
-    xy_near = [pltpu.make_async_copy(src, dst.at[own_rows, :], xy_loc.at[i]) for i, (src, dst) in enumerate(((xin, xbuf), (yin, ybuf)))]
+    xy_far = [remote(src, dst.at[own_rows, :], xy_send.at[i], xy_recv.at[i], (m, across)) for i, (src, dst) in enumerate(((xin, x_all), (yin, ybuf)))]
+    xy_near = [pltpu.make_async_copy(src, dst.at[own_rows, :], xy_loc.at[i]) for i, (src, dst) in enumerate(((xin, x_all), (yin, ybuf)))]
     for copy in xy_far + xy_near:
         copy.start()
     for copy in xy_near + xy_far:
@@ -124,10 +124,8 @@
     def strip_rows(i):
         return pl.ds(pl.multiple_of(i * STRIP, STRIP), STRIP)
 
-    stagings = (ebuf, eout)
-
     def master_copy(kind, q):
-        return pltpu.make_async_copy(piece(kind, a_own, c_own, q), stagings[q % 2].at[pl.ds(0, depth), :], stage_loc.at[q % 2])
+        return pltpu.make_async_copy(piece(kind, a_own, c_own, q), rem.at[q], stage_loc.at[q])
 
     def twin_copy(kind, q):
         ref = piece(kind, a, c, q)
@@ -138,8 +136,6 @@
 
     def load_weights(kind, scale):
         for q in range(4):
-            if scale is None or q >= 2:
-                master_copy(kind, q).start() if scale is not None else None
             if scale is None:
                 for shard in (2 * q, 2 * q + 1):
                     far = remote(weight_ends(kind, 0, shard)[0], weight_ends(kind, 0, shard)[1], w_send.at[0], w_recv.at[shard], (m, mine))
@@ -157,7 +153,7 @@
 
             def round_strip(i, carry):
                 dst, where = strip(kind, a, c, q, i)
-                value = stagings[q % 2][strip_rows(i), :]
+                value = rem[q, strip_rows(i), :]
                 if scale is not None:
                     src, _ = strip(kind, ga, gc, q, i)
                     value = value + scale * src[where]
@@ -178,7 +174,8 @@
         return remote(hout.at[block(mb), :], hbuf.at[block(mb), :], hs.at[mb], hr.at[mb], next_dev)
 
     def e_copy(mb):
-        return remote(eout.at[block(mb), :], ebuf.at[block(mb), :], es.at[mb], er.at[mb], prev_dev)
+        ref = ebuf.at[pl.ds(pl.multiple_of(mb * rows, rows), sent), :]
+        return remote(ref, ref, es.at[mb], er.at[mb], prev_dev)
 
     def forward(mb):
         h = hbuf[block(mb), :]
@@ -210,7 +207,7 @@
             zbuf[block(mb), sl] = dz
             part = dot(dz, a[:, sl], NT)
             back = part if back is None else back + part
-        eout[block(mb), :] = e + back
+        ebuf[block(mb), :] = e + back
 
     def grad_piece(shard, q):
         span = pl.ds(shard * shard_rows, shard_rows)
@@ -231,7 +228,9 @@
 
         @pl.when(stage == 0)
         def _():
-            hbuf[...] = xbuf[...]
+            x_copy = pltpu.make_async_copy(x_all, hbuf, w_loc)
+            x_copy.start()
+            x_copy.wait()
 
             @pl.when(core == 1)
             def _():
@@ -275,19 +274,19 @@
         def _():
             fold(loss_send)
             for step in range(32):
-                pltpu_copy = remote(loss_send, loss_out.at[core], l_send.at[step], l_recv.at[core], (step // 4, step % 4))
+                row_copy = remote(loss_send, loss_out.at[core], l_send.at[step], l_recv.at[core], (step // 4, step % 4))
 
                 @pl.when(here != step)
                 def _():
-                    pltpu_copy.start()
+                    row_copy.start()
 
             loss_out[core] = loss_send[...]
             for step in range(32):
-                pltpu_copy = remote(loss_send, loss_out.at[core], l_send.at[step], l_recv.at[core], (step // 4, step % 4))
+                row_copy = remote(loss_send, loss_out.at[core], l_send.at[step], l_recv.at[core], (step // 4, step % 4))
 
                 @pl.when(here != step)
                 def _():
-                    pltpu_copy.wait_send()
+                    row_copy.wait_send()
 
         def backward_step(mb):
             @pl.when(stage < 11)
@@ -303,9 +302,10 @@
             backward_step(mb)
             return carry
 
-        def second_shard(mb, carry):
-            backward_step(per_shard + mb)
-            grad_piece(0, mb)
+        def second_shard(q, carry):
+            for k in range(per_shard // 4):
+                backward_step(per_shard + q * (per_shard // 4) + k)
+            grad_piece(0, q)
             return carry
 
         def tail_grads(q, carry):
@@ -314,7 +314,7 @@
             return carry
 
         lax.fori_loop(0, per_shard, first_shard, 0)
-        lax.fori_loop(0, per_shard, second_shard, 0)
+        lax.fori_loop(0, 4, second_shard, 0)
         lax.fori_loop(0, 4, tail_grads, 0)
 
         def drain(mb, carry):
@@ -331,8 +331,6 @@
         lax.fori_loop(0, n_mb, drain, 0)
 
         def between(kind):
-            for q in range(2):
-                master_copy(kind, q).start()
             acc[...] = jnp.zeros_like(acc)
 
             def total_quarter(q, carry):
@@ -348,6 +346,8 @@
                 return lax.fori_loop(0, strips, total_strip, carry)
 
             lax.fori_loop(0, 4, total_quarter, 0)
+            for q in range(4):
+                master_copy(kind, q).start()
             fold(nrm_send)
             slot = stage * 2 + core
 
@@ -383,6 +383,7 @@
 
     @pl.when(active)
     def _():
+        ebuf[...] = jnp.zeros_like(ebuf)
         on_core(lambda kind: load_weights(kind, None))
         lax.fori_loop(0, 2, run_pass, 0)
 
@@ -483,7 +484,7 @@
             remote(loss_send, loss_out.at[k], l_send.at[0], l_recv.at[k], (m, mine)).wait_recv()
 
 
-def run_step(win, wout, xin, yin, rows, per_shard, res_scale, rho, n_data):
+def run_step(win, wout, xin, yin, rows, sent, per_shard, res_scale, rho, n_data):
     layers, depth, width = win.shape
     hidden = width * 8
     total = 2 * per_shard * rows
@@ -493,30 +494,28 @@
     f32, bf16 = jnp.float32, jnp.bfloat16
     any_space = pl.BlockSpec(memory_space=pl.ANY)
     return pl.pallas_call(
-        functools.partial(step_kernel, (rows, per_shard, n_mb, res_scale, rho, n_data)),
-        out_shape=[shape(win.shape, f32), shape(wout.shape, f32), shape((depth, hidden), f32), shape((hidden, depth), f32), shape((2, 8, 128), f32)],
+        functools.partial(step_kernel, (rows, sent, per_shard, n_mb, res_scale, rho, n_data)),
+        out_shape=[shape(win.shape, f32), shape(wout.shape, f32), shape((depth, hidden), f32), shape((hidden, depth), f32), shape((total, depth), bf16), shape((2, 8, 128), f32)],
         in_specs=[any_space] * 4,
-        out_specs=[any_space] * 4 + [pl.BlockSpec(memory_space=pltpu.VMEM)],
+        out_specs=[any_space] * 5 + [pl.BlockSpec(memory_space=pltpu.VMEM)],
         scratch_shapes=[
             pltpu.VMEM((depth, hidden), bf16),
             pltpu.VMEM((hidden, depth), bf16),
             pltpu.VMEM((depth, hidden), f32),
             pltpu.VMEM((hidden, depth), f32),
-            pltpu.VMEM((4, depth, hidden // 4), f32) if depth == hidden // 4 else pltpu.VMEM((4, depth, depth), f32),
-            pltpu.VMEM((total, depth), bf16),
+            pltpu.VMEM((4, depth, depth), f32),
             pltpu.VMEM((total, depth), bf16),
             pltpu.VMEM((total, depth), bf16),
             pltpu.VMEM((total, depth), bf16),
             pltpu.VMEM((total, hidden), bf16),
             pltpu.VMEM((total, hidden), bf16),
             pltpu.VMEM((total, depth), f32),
-            pltpu.VMEM((total, depth), f32),
             pltpu.VMEM((total, depth), bf16),
             pltpu.VMEM((1, depth), f32),
             pltpu.VMEM((8, 128), f32),
             pltpu.VMEM((24, 8, 128), f32),
             pltpu.VMEM((8, 128), f32),
-            dma((HALF,)), dma((8,)), dma, dma((2,)), dma((2,)), dma((2,)), dma((2,)), dma((4,)), dma((4,)), dma((4,)), dma((4,)),
+            dma((HALF,)), dma((8,)), dma, dma((2,)), dma((2,)), dma((2,)), dma((4,)), dma((4,)), dma((4,)), dma((4,)), dma((4,)),
             dma((n_mb,)), dma((n_mb,)), dma((n_mb,)), dma((n_mb,)), pltpu.SemaphoreType.REGULAR,
             dma((24,)), dma((24,)), dma((32,)), dma((2,)),
             dma((8,)), dma((HALF,)), dma((HALF,)), dma((HALF,)), dma((2 * HALF,)), dma((2 * HALF,)), dma,
@@ -540,6 +539,7 @@
             images, seq, depth = x_blk.shape
             raw = MB_IMAGES * seq
             rows = (raw + 15) // 16 * 16
+            sent = (raw + 7) // 8 * 8
             per_shard = images // MB_IMAGES
 
             def flat(blk):
@@ -547,7 +547,7 @@
                 return jnp.pad(mbs, ((0, 0), (0, rows - raw), (0, 0))).reshape(per_shard * rows, depth)
 
             res_scale = float(images * seq * depth)
-            grad_in, grad_out, _, _, loss = run_step(win_loc, wout_loc, flat(x_blk), flat(y_blk), rows, per_shard, res_scale, rho, n_data)
+            grad_in, grad_out, _, _, _, loss = run_step(win_loc, wout_loc, flat(x_blk), flat(y_blk), rows, sent, per_shard, res_scale, rho, n_data)
             loss_val = 0.5 * jnp.sum(loss[:, 0, :]) / elem_total
             return win_loc - ETA * grad_in, wout_loc - ETA * grad_out, loss_val
 

time: 1170 us -> 1090 us (0.932)
  Pallas kernels: 1130 us -> 1050 us
    pallas_call x1, Pallas kernels: 1130 us -> 1050 us  [run_step(): pl.pallas_call(functools.partial(step_kernel, (rows, sent, per_shard, n_m...]
where the time goes in v3:
time: 1090 us
  Pallas kernels  1050 us (96%)
  other arithmetic  28.2 us (3%)
    pallas_call x1, Pallas kernels, run_step(): pl.pallas_call(functools.partial(step_kernel, (rows, sent, per_shard, n_m...  1050 us
    sub x2, other arithmetic, local_step(): return (win_loc - ETA * grad_in, wout_loc - ETA * grad_out, loss_val)  26.9 us

profile of v3, /device:TPU:31, one launch (start us, length us, event | category | flops | bytes accessed | tf_op | source)
XLA Modules:
  0.0 1086.5 jit_solution(15135084281793868182)
XLA Ops:
  0.6 1.2 copy.9
  1.8 0.9 pad.7.clone
  2.8 1.2 copy.10
  3.9 0.9 pad.8.clone
  4.9 1048.8 %sam_step.1 = (f32[12,768,384]{2,1,0:T(8,128)}, f32[12,384,768]{2,1,0:T(8,128)}, f32[768,3072]{1,0:T(8,128)}, f32[3072,768]{1,0:T(8,128)}, bf16[1024,768]{1,0:T(8,128)(2,1)}, /*index=5*/f32[2,8,128]{2,1,0:T(8,128)}) custom-call(f32[12,768,384]{2,1,0:T(8,128)} %win.1, f32[12,384,768]{2,1,0:T(8,128)} %wout.1, bf16[512,768]{1,0:T(8,128)(2,1)} %bitcast.2, ...), custom_call_target="tpu_custom_call" | custom-call | tf_op jit(solution)/shard_map/sam_step/pallas_call | solution.py:496
  1053.6 1.3 slice_reduce_fusion
  1055.6 0.0 copy-start
  1055.6 15.4 %sub.6 = f32[12,768,384]{2,1,0:T(8,128)} subtract(f32[12,768,384]{2,1,0:T(8,128)} %win.1, f32[12,768,384]{2,1,0:T(8,128)} %get-tuple-element.6) | non-fusion elementwise | flops 3538944 | bytes 42467328 | tf_op jit(solution)/shard_map/sub | solution.py:552
  1071.0 2.8 copy-done
  1073.8 11.5 %sub.7 = f32[12,384,768]{2,1,0:T(8,128)} subtract(f32[12,384,768]{2,1,0:T(8,128)} %wout.1, f32[12,384,768]{2,1,0:T(8,128)S(1)} %copy-done) | non-fusion elementwise | flops 3538944 | bytes 42467328 | tf_op jit(solution)/shard_map/sub | solution.py:552
Async XLA Ops:
  1055.6 18.2 %copy-start = (f32[12,384,768]{2,1,0:T(8,128)S(1)}, f32[12,384,768]{2,1,0:T(8,128)}, u32[]{:S(2)}) copy-start(f32[12,384,768]{2,1,0:T(8,128)} %get-tuple-element.7) | copy-start | bytes 42467332

commit v4 on v3

--- a/solution.py
+++ b/solution.py
@@ -68,6 +68,10 @@
     prev_dev = stage_device(jnp.maximum(stage - 1, 0), core)
     next_dev = stage_device(jnp.minimum(stage + 1, 11), core)
     last = stage == 11
+    right = lax.div(m, 4)
+
+    def near_first(i):
+        return right * (3 - i) + (1 - right) * i
 
     def remote(src, dst, send, recv, dev):
         return pltpu.make_async_remote_copy(src, dst, send, recv, device_id=dev, device_id_type=MESH)
@@ -308,7 +312,8 @@
             grad_piece(0, q)
             return carry
 
-        def tail_grads(q, carry):
+        def tail_grads(i, carry):
+            q = near_first(i)
             grad_piece(1, q)
             on_core(lambda kind: grad_copy(1 - kind, q).start())
             return carry
@@ -409,12 +414,13 @@
 
         @pl.when(active)
         def _():
-            def send_quarter(q, carry):
+            def send_quarter(i, carry):
+                q = near_first(i)
                 grad_copy(kind, q).wait_recv()
 
-                def total_strip(i, carry):
-                    ref, where = strip(kind, ga, gc, q, i)
-                    ref[where] = (ref[where] + rem[q, strip_rows(i), :]) / n_data
+                def total_strip(j, carry):
+                    ref, where = strip(kind, ga, gc, q, j)
+                    ref[where] = (ref[where] + rem[q, strip_rows(j), :]) / n_data
                     return carry
 
                 lax.fori_loop(0, strips, total_strip, 0)

time: 1090 us -> 1010 us (0.927); the launches traced: 1090 us -> 993 us
  Pallas kernels: 1050 us -> 956 us
    pallas_call x1, Pallas kernels: 1050 us -> 956 us  [run_step(): pl.pallas_call(functools.partial(step_kernel, (rows, sent, per_shard, n_m...]
where the time goes in v4:
time: 1010 us; the launch traced here: 993 us
  Pallas kernels  956 us (95%)
  other arithmetic  28.2 us (3%)
    pallas_call x1, Pallas kernels, run_step(): pl.pallas_call(functools.partial(step_kernel, (rows, sent, per_shard, n_m...  956 us
    sub x2, other arithmetic, local_step(): return (win_loc - ETA * grad_in, wout_loc - ETA * grad_out, loss_val)  26.9 us

profile of v4, /device:TPU:31, one launch (start us, length us, event | category | flops | bytes accessed | tf_op | source)
XLA Modules:
  0.0 993.3 jit_solution(14703217217340967915)
XLA Ops:
  0.6 1.2 copy.9
  1.8 0.9 pad.7.clone
  2.8 1.2 copy.10
  3.9 0.9 pad.8.clone
  4.9 955.5 %sam_step.1 = (f32[12,768,384]{2,1,0:T(8,128)}, f32[12,384,768]{2,1,0:T(8,128)}, f32[768,3072]{1,0:T(8,128)}, f32[3072,768]{1,0:T(8,128)}, bf16[1024,768]{1,0:T(8,128)(2,1)}, /*index=5*/f32[2,8,128]{2,1,0:T(8,128)}) custom-call(f32[12,768,384]{2,1,0:T(8,128)} %win.1, f32[12,384,768]{2,1,0:T(8,128)} %wout.1, bf16[512,768]{1,0:T(8,128)(2,1)} %bitcast.2, ...), custom_call_target="tpu_custom_call" | custom-call | tf_op jit(solution)/shard_map/sam_step/pallas_call | solution.py:502
  960.4 1.3 slice_reduce_fusion
  962.4 0.0 copy-start
  962.4 15.4 %sub.6 = f32[12,768,384]{2,1,0:T(8,128)} subtract(f32[12,768,384]{2,1,0:T(8,128)} %win.1, f32[12,768,384]{2,1,0:T(8,128)} %get-tuple-element.6) | non-fusion elementwise | flops 3538944 | bytes 42467328 | tf_op jit(solution)/shard_map/sub | solution.py:558
  977.8 2.8 copy-done
  980.6 11.5 %sub.7 = f32[12,384,768]{2,1,0:T(8,128)} subtract(f32[12,384,768]{2,1,0:T(8,128)} %wout.1, f32[12,384,768]{2,1,0:T(8,128)S(1)} %copy-done) | non-fusion elementwise | flops 3538944 | bytes 42467328 | tf_op jit(solution)/shard_map/sub | solution.py:558
Async XLA Ops:
  962.4 18.2 %copy-start = (f32[12,384,768]{2,1,0:T(8,128)S(1)}, f32[12,384,768]{2,1,0:T(8,128)}, u32[]{:S(2)}) copy-start(f32[12,384,768]{2,1,0:T(8,128)} %get-tuple-element.7) | copy-start | bytes 42467332
